TPU v7x, 32 devices: a whole 2x2x4 slice. The times are simulated.
32 devices in a mesh: dom: 8 (over z, y), rep: 4 (over x, core).
Axes of the slice: x: 2, y: 2, z: 4, core: 2. Of those that a mesh axis runs over, the one named last changes fastest.
Arguments:
- ns_shape: bfloat16 [64, 256], replicated, may hold values from -0.75 to 0.75
- nm_shape: bfloat16 [64, 256], replicated, may hold values from -0.75 to 0.75
- sec_disp: bfloat16 [64, 262144], P(None, ('dom', 'rep')), may hold values from -6 to 6
- mst_disp: bfloat16 [64, 262144], P(None, ('dom', 'rep')), may hold values from -6 to 6
- gap_offset: float32 [262144], P(('dom', 'rep')), may hold values from -6 to 6
- quad_weight: float32 [256], replicated, may hold values from 0.25 to 4
- jacobian: float32 [262144], P(('dom', 'rep')), may hold values from 0.0005 to 0.005
- segment_slot: int32 [262144], P(('dom', 'rep')), may hold values from 0 to 1279, as said below
- face_id: int32 [262144], P(('dom', 'rep')), may hold values from 0 to 1073741823
- search_rank: int32 [262144], P(('dom', 'rep')), may hold values from 0 to 3
- live_rows: int32 [32], P(('dom', 'rep')), may hold values from 1024 to 8192, as said below
Outputs:
- contact_force: bfloat16 [64, 262144], P(None, ('dom', 'rep'))
- seg_pen: float32 [8192], P('dom')
- seg_face: int32 [8192], P('dom')
- seg_gap: float32 [8192], P('dom')
- mean_gap: float32 [], replicated
Inputs may be any that keep to these rules, and one draw needn't show every extreme that they name: `segment_slot`: A row's segment is (1024 times the dom index of its device plus its slot) modulo 8192; slots of 1024 or more reach the next dom index's first 256 segments. `live_rows`: entry b counts the live rows of the device with flat index b (dom-major); they are that device's first rows, the rest are padding; some device is full in every draw.
All inputs are finite; a program needn't handle non-finite values.
Results may differ from a plain program's by a relative error of at most 0.0055.
Values sent between devices are 32-bit elements; how exact they have to be, the bound alone decides.
A program may use at most 64 MiB of HBM per device.

v0:
```python
import math

import jax
import jax.numpy as jnp
from jax import lax
from jax.sharding import PartitionSpec as P

SEG_DEV = 1024
SPILL = 256


PENALTY = 400.0
LOWEST_FILL = -1e30
FACE_LIMIT = 1073741824


def combined_all(value, axis, join):
    pieces = jax.tree.map(lambda part: lax.all_gather(part, axis), value)
    head = jax.tree.map(lambda part: part[0], pieces)
    tail = jax.tree.map(lambda part: part[1:], pieces)
    running, _ = lax.scan(lambda running, share: (join(running, share), None), head, tail)
    return running


def passed_along(x, axis, by):
    length = lax.axis_size(axis)
    return lax.ppermute(x, axis, [(i, (i + by) % length) for i in range(length)])


def project(shape_table, displace):
    return lax.dot_general(
        shape_table, displace, (((0,), (0,)), ((), ())), preferred_element_type=jnp.float32
    )


def combine(earlier, latter):
    prefer = (latter[1] > earlier[1]) | (latter[1] == earlier[1]) & (latter[2] < earlier[2])
    head = (
        jnp.maximum(earlier[0], latter[0]),
        jnp.where(prefer, latter[1], earlier[1]),
        jnp.where(prefer, latter[2], earlier[2]),
    )
    return head + tuple(
        (left_part + right_part for left_part, right_part in zip(earlier[3:], latter[3:]))
    )


def window_stats(gap_field, jac_row, weights, slots, faces, ranks, live, window_len):
    row_pen = jnp.max(-gap_field, axis=0)
    row_gap = jac_row * jnp.dot(weights, gap_field, precision=lax.Precision.HIGHEST)
    row_area = jac_row * jnp.sum(weights)
    row_count = gap_field.shape[1]
    block_len = math.gcd(row_count, 1024)
    turns = row_count // block_len
    slot_ids = jnp.arange(window_len, dtype=jnp.int32)[:, None]
    paired = jnp.stack([row_gap, row_area], axis=0)

    def one_block(turn, carry):
        begin = turn * block_len

        def take(values):
            return lax.dynamic_slice_in_dim(values, begin, block_len, values.ndim - 1)

        block_live = take(live)
        block_ranks = take(ranks)
        member = slot_ids == take(slots)[None, :]
        hit = member & block_live[None, :]
        penalty_max = jnp.max(jnp.where(hit, take(row_pen)[None, :], LOWEST_FILL), axis=1)
        best_rank = jnp.max(jnp.where(hit, block_ranks[None, :], -1), axis=1)
        row_best = jnp.max(jnp.where(member, best_rank[:, None], -1), axis=0)
        chosen = jnp.where(block_live & (block_ranks == row_best), take(faces), FACE_LIMIT)
        lowest_face = jnp.min(jnp.where(member, chosen[None, :], FACE_LIMIT), axis=1)
        sums = lax.dot_general(
            take(paired),
            hit.astype(jnp.float32),
            (((1,), (1,)), ((), ())),
            precision=lax.Precision.HIGHEST,
        )
        fresh = (penalty_max, best_rank, lowest_face, sums[0], sums[1])
        return combine(carry, fresh)

    start = (
        jnp.full((window_len,), LOWEST_FILL, jnp.float32),
        jnp.full((window_len,), -1, jnp.int32),
        jnp.full((window_len,), FACE_LIMIT, jnp.int32),
        jnp.zeros((window_len,), jnp.float32),
        jnp.zeros((window_len,), jnp.float32),
    )
    return lax.fori_loop(0, turns, one_block, start)


def shards(
    ns_shape,
    nm_shape,
    sec_disp,
    mst_disp,
    gap_offset,
    quad_weight,
    jacobian,
    segment_slot,
    face_id,
    search_rank,
    live_rows,
):
    row_count = sec_disp.shape[1]
    window_len = SEG_DEV + SPILL
    gap_field = project(ns_shape, sec_disp) - project(nm_shape, mst_disp) + gap_offset[None, :]
    live = jnp.arange(row_count, dtype=jnp.int32) < live_rows[0]
    load = jnp.where(
        live[None, :],
        quad_weight[:, None] * jacobian[None, :] * PENALTY * jnp.maximum(-gap_field, 0.0),
        0.0,
    ).astype(jnp.bfloat16)
    contact_force = jnp.dot(ns_shape, load, preferred_element_type=jnp.float32).astype(jnp.bfloat16)
    stats = window_stats(
        gap_field, jacobian, quad_weight, segment_slot, face_id, search_rank, live, window_len
    )
    grouped = combined_all(stats, "rep", combine)
    spill = tuple((part[SEG_DEV:] for part in grouped))
    arrived = passed_along(spill, "dom", 1)
    leading = combine(tuple((part[:SPILL] for part in grouped)), arrived)
    own = tuple(
        (
            jnp.concatenate([lead_part, part[SPILL:SEG_DEV]])
            for lead_part, part in zip(leading, grouped)
        )
    )
    seg_pen = jnp.where(own[1] < 0, jnp.float32(0.0), own[0])
    seg_face = jnp.where(own[1] < 0, -1, own[2]).astype(jnp.int32)
    seg_gap = own[3]
    gap_total, area_total = lax.psum((jnp.sum(own[3]), jnp.sum(own[4])), "dom")
    mean_gap = gap_total / area_total
    return (contact_force, seg_pen, seg_face, seg_gap, mean_gap)


def solution(mesh):
    return jax.shard_map(
        shards,
        mesh=mesh,
        in_specs=(
            P(),
            P(),
            P(None, ("dom", "rep")),
            P(None, ("dom", "rep")),
            P(("dom", "rep")),
            P(),
            P(("dom", "rep")),
            P(("dom", "rep")),
            P(("dom", "rep")),
            P(("dom", "rep")),
            P(("dom", "rep")),
        ),
        out_specs=(P(None, ("dom", "rep")), P("dom"), P("dom"), P("dom"), P()),
        check_vma=False,
    )
```

profile of v0, /device:TPU:0, one launch (start us, length us, event | category | flops | bytes accessed | tf_op | source)
XLA Modules:
  0.0 163.1 jit_solution(12261108922890064860)
XLA Ops:
  1.5 5.7 %fusion.28 = f32[256,8192]{1,0:T(8,128)} fusion(bf16[64,256]{1,0:T(8,128)(2,1)} %param.15, bf16[64,8192]{1,0:T(8,128)(2,1)} %param.17), kind=kOutput, calls=%fused_computation.69 | convolution fusion | flops 268435456 | bytes 9469952 | tf_op jit(solution)/shard_map/dot_general | solution.py:31
  7.8 4.8 %negate_reduce_fusion = (f32[8192]{0:T(1024)S(1)}, f32[256,8192]{1,0:T(8,128)S(1)}) fusion(f32[8192]{0:T(1024)S(1)} %copy-done.2, f32[256,8192]{1,0:T(8,128)} %fusion.28, bf16[64,256]{1,0:T(8,128)(2,1)S(1)} %copy-done.3, bf16[64,8192]{1,0:T(8,128)(2,1)S(1)} %copy-done), kind=kOutput, calls=%fused_computation.38 | convolution fusion | flops 276815872 | bytes 17924096 | tf_op jit(solution)/shard_map/dot_general | solution.py:31
  12.7 3.2 %copy-done.1 = f32[256,8192]{1,0:T(8,128)} copy-done((f32[256,8192]{1,0:T(8,128)}, f32[256,8192]{1,0:T(8,128)S(1)}, u32[]{:S(2)}) %copy-start.1) | copy-done | bytes 8388632
  15.9 4.4 %fusion.29 = f32[1,8192]{1,0:T(1,128)S(1)} fusion(f32[256,8192]{1,0:T(8,128)S(1)} %get-tuple-element.406, f32[256,1]{0,1:T(1,128)S(1)} %bitcast.38), kind=kOutput, calls=%fused_computation.70 | convolution fusion | flops 25165824 | bytes 8422400 | tf_op jit(solution)/shard_map/dot_general | solution.py:50
  21.0 70.1 %while.41 = (s32[]{:T(128)}, f32[1280]{0:T(1024)S(1)}, s32[1280]{0:T(1024)S(1)}, s32[1280]{0:T(1024)S(1)}, f32[1280]{0:T(1024)S(1)}, /*index=5*/f32[1280]{0:T(10...) while((s32[]{:T(128)}, f32[1280]{0:T(1024)S(1)}, ...), condition=%wide.region_7.8_spmd.clone, body=%wide.region_2.7_spmd.clone.sunk | while | flops 52446216 | bytes 220391 | solution.py:89
  21.9 2.5 %fusion.54 = f32[2,1280]{1,0:T(2,128)S(1)} fusion(s32[1024]{0:T(1024)S(1)} %dynamic_slice.94, pred[1024]{0:T(1024)(128)(4,1)S(1)} %dynamic_slice.95, f32[2,8192]{1,0:T(2,128)S(1)} %get-tuple-element.615, s32[]{:T(128)S(6)} %select_n.142), kind=kOutput, calls=%fused_computation.13.clone.1 | convolution fusion | flops 34078720 | bytes 23556 | tf_op jit(solution)/shard_map/while/body/eval_jaxpr/dot_general | solution.py:73
  25.2 1.3 fusion.50
  26.5 0.8 fusion.51
  28.8 1.1 fusion.49
  30.7 2.5 %fusion.54 = f32[2,1280]{1,0:T(2,128)S(1)} fusion(s32[1024]{0:T(1024)S(1)} %dynamic_slice.94, pred[1024]{0:T(1024)(128)(4,1)S(1)} %dynamic_slice.95, f32[2,8192]{1,0:T(2,128)S(1)} %get-tuple-element.615, s32[]{:T(128)S(6)} %select_n.142), kind=kOutput, calls=%fused_computation.13.clone.1 | convolution fusion | flops 34078720 | bytes 23556 | tf_op jit(solution)/shard_map/while/body/eval_jaxpr/dot_general | solution.py:73
  34.0 1.3 fusion.50
  35.3 0.8 fusion.51
  37.6 1.1 fusion.49
  39.4 2.5 %fusion.54 = f32[2,1280]{1,0:T(2,128)S(1)} fusion(s32[1024]{0:T(1024)S(1)} %dynamic_slice.94, pred[1024]{0:T(1024)(128)(4,1)S(1)} %dynamic_slice.95, f32[2,8192]{1,0:T(2,128)S(1)} %get-tuple-element.615, s32[]{:T(128)S(6)} %select_n.142), kind=kOutput, calls=%fused_computation.13.clone.1 | convolution fusion | flops 34078720 | bytes 23556 | tf_op jit(solution)/shard_map/while/body/eval_jaxpr/dot_general | solution.py:73
  42.7 1.3 fusion.50
  44.0 0.8 fusion.51
  46.3 1.1 fusion.49
  48.2 2.5 %fusion.54 = f32[2,1280]{1,0:T(2,128)S(1)} fusion(s32[1024]{0:T(1024)S(1)} %dynamic_slice.94, pred[1024]{0:T(1024)(128)(4,1)S(1)} %dynamic_slice.95, f32[2,8192]{1,0:T(2,128)S(1)} %get-tuple-element.615, s32[]{:T(128)S(6)} %select_n.142), kind=kOutput, calls=%fused_computation.13.clone.1 | convolution fusion | flops 34078720 | bytes 23556 | tf_op jit(solution)/shard_map/while/body/eval_jaxpr/dot_general | solution.py:73
  51.5 1.3 fusion.50
  52.7 0.8 fusion.51
  55.1 1.1 fusion.49
  56.9 2.5 %fusion.54 = f32[2,1280]{1,0:T(2,128)S(1)} fusion(s32[1024]{0:T(1024)S(1)} %dynamic_slice.94, pred[1024]{0:T(1024)(128)(4,1)S(1)} %dynamic_slice.95, f32[2,8192]{1,0:T(2,128)S(1)} %get-tuple-element.615, s32[]{:T(128)S(6)} %select_n.142), kind=kOutput, calls=%fused_computation.13.clone.1 | convolution fusion | flops 34078720 | bytes 23556 | tf_op jit(solution)/shard_map/while/body/eval_jaxpr/dot_general | solution.py:73
  60.2 1.3 fusion.50
  61.5 0.8 fusion.51
  63.8 1.1 fusion.49
  65.6 2.5 %fusion.54 = f32[2,1280]{1,0:T(2,128)S(1)} fusion(s32[1024]{0:T(1024)S(1)} %dynamic_slice.94, pred[1024]{0:T(1024)(128)(4,1)S(1)} %dynamic_slice.95, f32[2,8192]{1,0:T(2,128)S(1)} %get-tuple-element.615, s32[]{:T(128)S(6)} %select_n.142), kind=kOutput, calls=%fused_computation.13.clone.1 | convolution fusion | flops 34078720 | bytes 23556 | tf_op jit(solution)/shard_map/while/body/eval_jaxpr/dot_general | solution.py:73
  69.0 1.3 fusion.50
  70.2 0.8 fusion.51
  72.6 1.1 fusion.49
  74.4 2.5 %fusion.54 = f32[2,1280]{1,0:T(2,128)S(1)} fusion(s32[1024]{0:T(1024)S(1)} %dynamic_slice.94, pred[1024]{0:T(1024)(128)(4,1)S(1)} %dynamic_slice.95, f32[2,8192]{1,0:T(2,128)S(1)} %get-tuple-element.615, s32[]{:T(128)S(6)} %select_n.142), kind=kOutput, calls=%fused_computation.13.clone.1 | convolution fusion | flops 34078720 | bytes 23556 | tf_op jit(solution)/shard_map/while/body/eval_jaxpr/dot_general | solution.py:73
  77.7 1.3 fusion.50
  81.3 1.1 fusion.49
  83.1 2.5 %fusion.54 = f32[2,1280]{1,0:T(2,128)S(1)} fusion(s32[1024]{0:T(1024)S(1)} %dynamic_slice.94, pred[1024]{0:T(1024)(128)(4,1)S(1)} %dynamic_slice.95, f32[2,8192]{1,0:T(2,128)S(1)} %get-tuple-element.615, s32[]{:T(128)S(6)} %select_n.142), kind=kOutput, calls=%fused_computation.13.clone.1 | convolution fusion | flops 34078720 | bytes 23556 | tf_op jit(solution)/shard_map/while/body/eval_jaxpr/dot_general | solution.py:73
  86.5 1.3 fusion.50
  87.7 0.8 fusion.51
  90.0 1.1 fusion.49
  91.2 6.2 %all-gather.9 = f32[4,1,1280]{2,1,0:T(1,128)S(1)} all-gather(f32[1,1,1280]{2,1,0:T(1,128)S(1)} %reshape.51), channel_id=6, replica_groups=mesh['dom'=8,'rep'=4] {'rep'}, dimensions={0}, use_global_device_ids=true | all-gather | bytes 25600 | tf_op jit(solution)/shard_map/all_gather | solution.py:18
  97.5 5.4 %all-gather.8 = f32[4,1,1280]{2,1,0:T(1,128)S(1)} all-gather(f32[1,1,1280]{2,1,0:T(1,128)S(1)} %reshape.49), channel_id=5, replica_groups=mesh['dom'=8,'rep'=4] {'rep'}, dimensions={0}, use_global_device_ids=true | all-gather | bytes 25600 | tf_op jit(solution)/shard_map/all_gather | solution.py:18
  103.0 5.2 %all-gather.7 = s32[4,1,1280]{2,1,0:T(1,128)S(1)} all-gather(s32[1,1,1280]{2,1,0:T(1,128)S(1)} %reshape.47), channel_id=4, replica_groups=mesh['dom'=8,'rep'=4] {'rep'}, dimensions={0}, use_global_device_ids=true | all-gather | bytes 25600 | tf_op jit(solution)/shard_map/all_gather | solution.py:18
  108.2 5.2 %all-gather.6 = s32[4,1,1280]{2,1,0:T(1,128)S(1)} all-gather(s32[1,1,1280]{2,1,0:T(1,128)S(1)} %reshape.45), channel_id=3, replica_groups=mesh['dom'=8,'rep'=4] {'rep'}, dimensions={0}, use_global_device_ids=true | all-gather | bytes 25600 | tf_op jit(solution)/shard_map/all_gather | solution.py:18
  113.5 5.2 %all-gather.5 = f32[4,1,1280]{2,1,0:T(1,128)S(1)} all-gather(f32[1,1,1280]{2,1,0:T(1,128)S(1)} %reshape.43), channel_id=2, replica_groups=mesh['dom'=8,'rep'=4] {'rep'}, dimensions={0}, use_global_device_ids=true | all-gather | bytes 25600 | tf_op jit(solution)/shard_map/all_gather | solution.py:18
  119.4 1.8 %collective-permute-start.4 = (f32[256]{0:T(256)S(1)}, f32[256]{0:T(256)S(1)}, u32[]{:S(2)}, u32[]{:S(2)}) collective-permute-start(f32[256]{0:T(256)S(1)} %slice.112), channel_id=1, source_target_pairs={{0,4},{4,8},{8,12},{12,16},{16,20},{20,24},{24,28},{28,0},{1,5},{5... | collective-permute-start | bytes 3080 | tf_op jit(solution)/shard_map/ppermute | solution.py:27
  121.1 1.5 collective-permute-start.3
  122.7 1.5 collective-permute-start.2
  124.2 1.5 collective-permute-start
  125.7 1.5 collective-permute-start.1
  127.2 6.3 %fusion.22 = bf16[64,8192]{1,0:T(8,128)(2,1)} fusion(bf16[64,256]{1,0:T(8,128)(2,1)S(1)} %copy-done.4, f32[256,8192]{1,0:T(8,128)} %copy-done.1, f32[8192]{0:T(1024)S(1)} %copy-done.5, f32[256]{0:T(256)S(1)} %copy-done.6, pred[8192]{0:T(1024)(128)(4,1)S(1)} %get-tuple-element.656), kind=kOutput, calls=%fused_computation.36 | convolution fusion | flops 283639808 | bytes 9511936 | tf_op jit(solution)/shard_map/dot_general | solution.py:114
  139.2 20.8 %all-reduce = (f32[]{:T(128)}, f32[]{:T(128)}) all-reduce(f32[]{:T(128)S(6)} %reduce_sum.46, f32[]{:T(128)S(6)} %reduce_sum.49), channel_id=1, replica_groups=mesh['dom'=8,'rep'=4] {'dom'}, use_global_device_ids=true, to_apply=%region_12.13 | all-reduce | flops 2 | bytes 16 | tf_op jit(solution)/shard_map/psum | solution.py:131
  (167 shorter events, 30.6 us)
Async XLA Ops:
  0.6 7.2 %copy-start = (bf16[64,8192]{1,0:T(8,128)(2,1)S(1)}, bf16[64,8192]{1,0:T(8,128)(2,1)}, u32[]{:S(2)}) copy-start(bf16[64,8192]{1,0:T(8,128)(2,1)} %param.18) | copy-start | bytes 3145732
  0.6 6.6 %copy-start.6 = (f32[256]{0:T(256)S(1)}, f32[256]{0:T(256)}, u32[]{:S(2)}) copy-start(f32[256]{0:T(256)} %param.20) | copy-start | bytes 3076
  0.7 7.2 %copy-start.3 = (bf16[64,256]{1,0:T(8,128)(2,1)S(1)}, bf16[64,256]{1,0:T(8,128)(2,1)}, u32[]{:S(2)}) copy-start(bf16[64,256]{1,0:T(8,128)(2,1)} %param.16) | copy-start | bytes 98308
  0.7 7.1 %copy-start.2 = (f32[8192]{0:T(1024)S(1)}, f32[8192]{0:T(1024)}, u32[]{:S(2)}) copy-start(f32[8192]{0:T(1024)} %param.19) | copy-start | bytes 98308
  12.6 3.2 %copy-start.1 = (f32[256,8192]{1,0:T(8,128)}, f32[256,8192]{1,0:T(8,128)S(1)}, u32[]{:S(2)}) copy-start(f32[256,8192]{1,0:T(8,128)S(1)} %get-tuple-element.406) | copy-start | bytes 25165828
  12.6 7.6 %copy-start.5 = (f32[8192]{0:T(1024)S(1)}, f32[8192]{0:T(1024)}, u32[]{:S(2)}) copy-start(f32[8192]{0:T(1024)} %param.21) | copy-start | bytes 98308
  21.0 106.2 %copy-start.4 = (bf16[64,256]{1,0:T(8,128)(2,1)S(1)}, bf16[64,256]{1,0:T(8,128)(2,1)}, u32[]{:S(2)}) copy-start(bf16[64,256]{1,0:T(8,128)(2,1)} %param.15) | copy-start | bytes 98308
  119.4 15.4 %collective-permute-start.4 = (f32[256]{0:T(256)S(1)}, f32[256]{0:T(256)S(1)}, u32[]{:S(2)}, u32[]{:S(2)}) collective-permute-start(f32[256]{0:T(256)S(1)} %slice.112), channel_id=1, source_target_pairs={{0,4},{4,8},{8,12},{12,16},{16,20},{20,24},{24,28},{28,0},{1,5},{5... | collective-permute-start | bytes 3080 | tf_op jit(solution)/shard_map/ppermute | solution.py:27
  121.1 13.0 %collective-permute-start.3 = (f32[256]{0:T(256)S(1)}, f32[256]{0:T(256)S(1)}, u32[]{:S(2)}, u32[]{:S(2)}) collective-permute-start(f32[256]{0:T(256)S(1)} %slice.109), channel_id=1, source_target_pairs={{0,4},{4,8},{8,12},{12,16},{16,20},{20,24},{24,28},{28,0},{1,5},{5... | collective-permute-start | bytes 3080 | tf_op jit(solution)/shard_map/ppermute | solution.py:27
  122.7 38.7 %collective-permute-start.2 = (f32[256]{0:T(256)S(1)}, f32[256]{0:T(256)S(1)}, u32[]{:S(2)}, u32[]{:S(2)}) collective-permute-start(f32[256]{0:T(256)S(1)} %slice.105), channel_id=1, source_target_pairs={{0,4},{4,8},{8,12},{12,16},{16,20},{20,24},{24,28},{28,0},{1,5},{5... | collective-permute-start | bytes 3080 | tf_op jit(solution)/shard_map/ppermute | solution.py:27
  124.2 13.7 %collective-permute-start = (s32[256]{0:T(256)S(1)}, s32[256]{0:T(256)S(1)}, u32[]{:S(2)}, u32[]{:S(2)}) collective-permute-start(s32[256]{0:T(256)S(1)} %slice.99), channel_id=1, source_target_pairs={{0,4},{4,8},{8,12},{12,16},{16,20},{20,24},{24,28},{28,0},{1,5},{5... | collective-permute-start | bytes 3080 | tf_op jit(solution)/shard_map/ppermute | solution.py:27
  125.7 12.2 %collective-permute-start.1 = (s32[256]{0:T(256)S(1)}, s32[256]{0:T(256)S(1)}, u32[]{:S(2)}, u32[]{:S(2)}) collective-permute-start(s32[256]{0:T(256)S(1)} %slice.101), channel_id=1, source_target_pairs={{0,4},{4,8},{8,12},{12,16},{16,20},{20,24},{24,28},{28,0},{1,5},{5... | collective-permute-start | bytes 3080 | tf_op jit(solution)/shard_map/ppermute | solution.py:27
where the time goes:
time: 164 us; the launch traced here: 163 us
  blocking collectives  48.1 us (29%)
  other arithmetic  42.5 us (26%)
  matrix products  41.6 us (25%)
  local copies, waits for them, and re-layouts  15.3 us (9%)
  starting transfers between devices  7.87 us (5%)
  between operations  6.72 us (4%)
    all_gather x5, blocking collectives, combined_all(): pieces = jax.tree.map(lambda part: lax.all_gather(part, axis), value)  27.3 us
    psum x1, blocking collectives, shards(): gap_total, area_total = lax.psum((jnp.sum(own[3]), jnp.sum(own[4])), 'dom')  20.8 us
    dot_general x8, matrix products, one_block(): lax.dot_general(take(paired), hit.astype(jnp.float32), (((1,), (1,)), (()...  20.4 us
    dynamic_slice x32, local copies, waits for them, and re-layouts, take(): return lax.dynamic_slice_in_dim(values, begin, block_len, values.ndim - 1)  11.2 us
    dot_general x2, matrix products, project(): lax.dot_general(shape_table, displace, (((0,), (0,)), ((), ())), preferre...  10.5 us
    reduce_max x8, other arithmetic, one_block(): best_rank = jnp.max(jnp.where(hit, block_ranks[None, :], -1), axis=1)  10.2 us
    reduce_max x8, other arithmetic, one_block(): jnp.max(jnp.where(hit, take(row_pen)[None, :], LOWEST_FILL), axis=1)  8.89 us
    ppermute x5, starting transfers between devices, passed_along(): lax.ppermute(x, axis, [(i, (i + by) % length) for i in range(length)])  7.87 us
  transfers between devices with their start and end apart: 5, of which 0 were waited for; matrix products, arithmetic and copies ran while one was open for 6% of the time, Pallas kernels for 0%

commit v1 on v0

v1 whole, which is shorter than its diff:
```python
import functools

import jax
import jax.numpy as jnp
from jax import lax
from jax.experimental import pallas as pl
from jax.experimental.pallas import tpu as pltpu
from jax.sharding import PartitionSpec as P

SEG_DEV = 1024
SPILL = 256
LANES = 128
SUB = 8
GROUPS = (SEG_DEV + SPILL) // LANES
OWN_GROUPS = SEG_DEV // LANES
PAD_GROUPS = 16

PENALTY = 400.0
LOWEST_FILL = -1e30
FACE_LIMIT = 1073741824
FACE_MASK = FACE_LIMIT - 1
KEY_LOW = -2147483648
MESH = pl.DeviceIdType.MESH
TILE = 256


def split3(x):
    a = x.astype(jnp.bfloat16)
    rest = x - a.astype(jnp.float32)
    b = rest.astype(jnp.bfloat16)
    c = (rest - b.astype(jnp.float32)).astype(jnp.bfloat16)
    return a, b, c


def dense_kernel(
    live_ref, ns_ref, nm_ref, qw_ref, sec_ref, mst_ref, off_ref, jac_ref, slot_ref,
    force_ref, pen_ref, seg_ref,
    wt_ref, qcol_ref, qsum_ref,
):
    step = pl.program_id(0)
    k_size, p_size = ns_ref.shape
    rows = sec_ref.shape[1]
    lines = rows // LANES
    per_tile = TILE // LANES

    @pl.when(step == 0)
    def _():
        w = jnp.concatenate([ns_ref[...], -nm_ref[...]], axis=0).astype(jnp.float32)
        qrow = qw_ref[...]
        wt = w.T
        wt_ref[0:p_size, :] = wt.astype(jnp.bfloat16)
        qmat = jnp.broadcast_to(qrow, (LANES, p_size)).T
        qcol_ref[...] = qmat
        v = jnp.sum(wt * qmat, axis=0, keepdims=True)
        a, b, c = split3(v)
        pick = lax.broadcasted_iota(jnp.int32, (16, 2 * k_size), 0)
        stacked = jnp.where(
            pick == 0,
            a.astype(jnp.float32),
            jnp.where(pick == 1, b.astype(jnp.float32), jnp.where(pick == 2, c.astype(jnp.float32), 0.0)),
        )
        wt_ref[p_size:, :] = stacked.astype(jnp.bfloat16)
        qsum_ref[...] = jnp.broadcast_to(jnp.sum(qmat, axis=0, keepdims=True), (SUB, LANES))
        seg_ref[...] = jnp.zeros_like(seg_ref)

    live_count = live_ref[0]
    first = step * rows
    qcol = qcol_ref[...]
    qsum = qsum_ref[0:1, :]
    wt = wt_ref[...]
    ns = ns_ref[...]
    lane = lax.broadcasted_iota(jnp.int32, (1, LANES), 1)
    seg_total = jnp.zeros((PAD_GROUPS, LANES), jnp.float32)
    for tile in range(rows // TILE):
        cols = pl.ds(tile * TILE, TILE)
        x = jnp.concatenate([sec_ref[:, cols], mst_ref[:, cols]], axis=0)
        field = jnp.dot(wt, x, preferred_element_type=jnp.float32)
        pieces = []
        scales = []
        for part in range(per_tile):
            line = tile * per_tile + part
            here = slice(part * LANES, (part + 1) * LANES)
            offset = off_ref[line : line + 1, :]
            live = (lane + (first + line * LANES)) < live_count
            jac = jac_ref[line : line + 1, :]
            jac_live = jnp.where(live, jac, 0.0)
            gap = field[:p_size, here] + offset
            lowest = jnp.min(gap, axis=0, keepdims=True)
            pen_ref[line : line + 1, :] = jnp.where(live, -lowest, LOWEST_FILL)
            pieces.append((qcol * jnp.maximum(-gap, 0.0)).astype(jnp.bfloat16))
            scales.append(jac_live * PENALTY)
            summed = jnp.sum(field[p_size : p_size + SUB, here], axis=0, keepdims=True)
            row_gap = jac_live * (summed + offset * qsum)
            slot = slot_ref[line : line + 1, :]
            hi = slot >> 7
            lo = slot & (LANES - 1)
            hit_hi = lax.broadcasted_iota(jnp.int32, (PAD_GROUPS, LANES), 0) == hi
            hit_lo = lax.broadcasted_iota(jnp.int32, (LANES, LANES), 0) == lo
            spread = jnp.where(hit_hi, row_gap, 0.0)
            a, b, c = split3(spread)
            left = jnp.concatenate([a, b, c], axis=0)
            right = jnp.where(hit_lo, 1.0, 0.0).astype(jnp.bfloat16)
            got = lax.dot_general(
                left, right, (((1,), (1,)), ((), ())), preferred_element_type=jnp.float32
            )
            seg_total = seg_total + (
                got[0:PAD_GROUPS] + got[PAD_GROUPS : 2 * PAD_GROUPS] + got[2 * PAD_GROUPS :]
            )
        load = jnp.concatenate(pieces, axis=1)
        force = jnp.dot(ns, load, preferred_element_type=jnp.float32)
        force_ref[:, cols] = (force * jnp.concatenate(scales, axis=1)).astype(jnp.bfloat16)
    seg_ref[...] += seg_total


def merge_kernel(
    n_dom, n_rep,
    live_ref, qw_ref, slot_ref, face_ref, rank_ref, pen_ref, jac_ref, seg_ref,
    out_pen, out_face, out_gap, out_mean,
    pen_g, key_g, acc_pen, acc_key,
    sp_f, sp_i, ow_f, ow_i, tot_d, tot_r, tot_s,
    spill_f, spill_i, spill_t, own_f, own_i, own_t,
    s_spf, r_spf, s_spi, r_spi, s_owf, r_owf, s_owi, r_owi, s_td, r_td, s_tr, r_tr,
):
    dom = lax.axis_index("dom")
    rep = lax.axis_index("rep")
    lines = slot_ref.shape[0]

    def dev(d, r):
        return {"dom": lax.rem(d + n_dom, n_dom), "rep": lax.rem(r + n_rep, n_rep)}

    barrier = pltpu.get_barrier_semaphore()

    def greet(d, r):
        pl.semaphore_signal(barrier, inc=1, device_id=dev(d, r), device_id_type=MESH)

    for j in range(1, n_rep):
        greet(dom, rep + j)
        greet(dom + 1, rep + j)
        greet(dom - 1, rep + j)

    def greet_dom(j, carry):
        greet(dom + j, rep)
        return carry

    lax.fori_loop(1, n_dom, greet_dom, 0)

    live_count = live_ref[0]
    row_id = (
        lax.broadcasted_iota(jnp.int32, (lines, LANES), 0) * LANES
        + lax.broadcasted_iota(jnp.int32, (lines, LANES), 1)
    )
    live = row_id < live_count
    slot = slot_ref[...]
    hi = slot >> 7
    key = jnp.where(
        live, ((rank_ref[...] - 2) << 30) + (FACE_MASK - face_ref[...]), KEY_LOW
    )
    pen = pen_ref[...]
    for g in range(GROUPS):
        inside = hi == g
        pen_g[g * lines : (g + 1) * lines, :] = jnp.where(inside, pen, LOWEST_FILL)
        key_g[g * lines : (g + 1) * lines, :] = jnp.where(inside, key, KEY_LOW)

    total_gap = jnp.sum(jnp.sum(seg_ref[...], axis=0, keepdims=True), axis=1, keepdims=True)
    area_rows = jnp.where(live, jac_ref[...], 0.0)
    total_area = jnp.sum(
        jnp.sum(area_rows, axis=0, keepdims=True), axis=1, keepdims=True
    ) * jnp.sum(qw_ref[...], axis=1, keepdims=True)
    sub = lax.broadcasted_iota(jnp.int32, (SUB, LANES), 0)
    pair = jnp.where(sub == 0, total_gap, jnp.where(sub == 1, total_area, 0.0))
    tot_s[...] = pair
    tot_d[dom] = pair

    pl.semaphore_wait(barrier, 3 * (n_rep - 1) + n_dom - 1)

    def tot_dom(j):
        return pltpu.make_async_remote_copy(
            src_ref=tot_s, dst_ref=tot_d.at[dom],
            send_sem=s_td.at[j], recv_sem=r_td.at[dom],
            device_id=dev(dom + j, rep), device_id_type=MESH,
        )

    def tot_dom_in(j):
        source = lax.rem(dom - j + n_dom, n_dom)
        return pltpu.make_async_remote_copy(
            src_ref=tot_s, dst_ref=tot_d.at[source],
            send_sem=s_td.at[j], recv_sem=r_td.at[source],
            device_id=dev(dom + j, rep), device_id_type=MESH,
        )

    def start_tot(j, carry):
        tot_dom(j).start()
        return carry

    lax.fori_loop(1, n_dom, start_tot, 0)

    def scan_groups(g0, g1, per):
        count = g1 - g0
        width = SUB * per

        def one(block, carry):
            base = block * width
            marks = [
                lax.broadcasted_iota(jnp.int32, (SUB, LANES), 0) + (base + SUB * q)
                for q in range(per)
            ]

            def body(i, accs):
                accs = list(accs)
                c = i
                lo = slot_ref[pl.ds(c, SUB, stride=0), :] & (LANES - 1)
                hits = [lo == m for m in marks]
                for g in range(count):
                    at = (g0 + g) * lines + c
                    pv = pen_g[pl.ds(at, SUB, stride=0), :]
                    kv = key_g[pl.ds(at, SUB, stride=0), :]
                    for q in range(per):
                        n = 2 * (g * per + q)
                        accs[n] = jnp.maximum(accs[n], jnp.where(hits[q], pv, LOWEST_FILL))
                        accs[n + 1] = jnp.maximum(accs[n + 1], jnp.where(hits[q], kv, KEY_LOW))
                return tuple(accs)

            start = (
                jnp.full((SUB, LANES), LOWEST_FILL, jnp.float32),
                jnp.full((SUB, LANES), KEY_LOW, jnp.int32),
            ) * (count * per)
            accs = lax.fori_loop(0, lines, body, start, unroll=4)
            for g in range(count):
                for q in range(per):
                    n = 2 * (g * per + q)
                    rows = pl.ds((g0 + g) * LANES + base + SUB * q, SUB)
                    acc_pen[rows, :] = accs[n]
                    acc_key[rows, :] = accs[n + 1]
            return carry

        lax.fori_loop(0, LANES // width, one, 0)

    def gather_group(g):
        rows = pl.ds(g * LANES, LANES)
        top = jnp.max(acc_pen[rows, :].T, axis=0, keepdims=True)
        best = jnp.max(acc_key[rows, :].T, axis=0, keepdims=True)
        return top, best

    def decode(top, best):
        none = top < LOWEST_FILL * 0.5
        rank = jnp.where(none, -1, (best >> 30) + 2)
        face = jnp.where(none, FACE_LIMIT, FACE_MASK - (best & FACE_MASK))
        return rank, face

    scan_groups(OWN_GROUPS, GROUPS, 4)
    spill_f[0] = jnp.full((SUB, LANES), LOWEST_FILL, jnp.float32)
    spill_i[0] = jnp.full((SUB, LANES), -1, jnp.int32)
    spill_i[1] = jnp.full((SUB, LANES), FACE_LIMIT, jnp.int32)
    spill_f[1] = seg_ref[OWN_GROUPS:, :]
    for g in range(OWN_GROUPS, GROUPS):
        top, best = gather_group(g)
        rank, face = decode(top, best)
        at = pl.ds(g - OWN_GROUPS, 1)
        spill_f[0, at, :] = top
        spill_i[0, at, :] = rank
        spill_i[1, at, :] = face

    def spill_copy(j, source):
        return (
            pltpu.make_async_remote_copy(
                src_ref=spill_f, dst_ref=sp_f.at[source],
                send_sem=s_spf.at[j], recv_sem=r_spf.at[source],
                device_id=dev(dom + 1, rep + j), device_id_type=MESH,
            ),
            pltpu.make_async_remote_copy(
                src_ref=spill_i, dst_ref=sp_i.at[source],
                send_sem=s_spi.at[j], recv_sem=r_spi.at[source],
                device_id=dev(dom + 1, rep + j), device_id_type=MESH,
            ),
        )

    for j in range(n_rep):
        for copy in spill_copy(j, rep):
            copy.start()

    def wait_tot(j, carry):
        tot_dom_in(j).wait_recv()
        return carry

    lax.fori_loop(1, n_dom, wait_tot, 0)

    def add_tot(j, total):
        return total + tot_d[j]

    dom_total = lax.fori_loop(0, n_dom, add_tot, jnp.zeros((SUB, LANES), jnp.float32))
    own_t[...] = dom_total
    tot_r[rep] = dom_total

    def rep_tot(j, source):
        return pltpu.make_async_remote_copy(
            src_ref=own_t, dst_ref=tot_r.at[source],
            send_sem=s_tr.at[j], recv_sem=r_tr.at[source],
            device_id=dev(dom, rep + j), device_id_type=MESH,
        )

    for j in range(1, n_rep):
        rep_tot(j, rep).start()

    scan_groups(0, OWN_GROUPS, 2)
    own_f[1] = seg_ref[:OWN_GROUPS, :]
    for g in range(OWN_GROUPS):
        top, best = gather_group(g)
        rank, face = decode(top, best)
        at = pl.ds(g, 1)
        own_f[0, at, :] = top
        own_i[0, at, :] = rank
        own_i[1, at, :] = face

    def own_copy(j, source):
        return (
            pltpu.make_async_remote_copy(
                src_ref=own_f, dst_ref=ow_f.at[source],
                send_sem=s_owf.at[j], recv_sem=r_owf.at[source],
                device_id=dev(dom, rep + j), device_id_type=MESH,
            ),
            pltpu.make_async_remote_copy(
                src_ref=own_i, dst_ref=ow_i.at[source],
                send_sem=s_owi.at[j], recv_sem=r_owi.at[source],
                device_id=dev(dom, rep + j), device_id_type=MESH,
            ),
        )

    for j in range(1, n_rep):
        for copy in own_copy(j, rep):
            copy.start()
    ow_f[rep] = own_f[...]
    ow_i[rep] = own_i[...]

    def encode(rank, face):
        return jnp.where(rank < 0, KEY_LOW, ((rank - 2) << 30) + (FACE_MASK - face))

    for j in range(1, n_rep):
        rep_tot(j, lax.rem(rep - j + n_rep, n_rep)).wait_recv()
    whole = tot_r[0]
    for r in range(1, n_rep):
        whole = whole + tot_r[r]
    out_mean[0] = jnp.sum(whole[0:1, 0:1]) / jnp.sum(whole[1:2, 0:1])

    for j in range(n_rep):
        for copy in spill_copy(j, lax.rem(rep - j + n_rep, n_rep)):
            copy.wait_recv()
    pen_s, gap_s = sp_f[0, 0], sp_f[0, 1]
    key_s = encode(sp_i[0, 0], sp_i[0, 1])
    for r in range(1, n_rep):
        pen_s = jnp.maximum(pen_s, sp_f[r, 0])
        gap_s = gap_s + sp_f[r, 1]
        key_s = jnp.maximum(key_s, encode(sp_i[r, 0], sp_i[r, 1]))
    for j in range(1, n_rep):
        for copy in own_copy(j, lax.rem(rep - j + n_rep, n_rep)):
            copy.wait_recv()
    pen_o, key_o, gap_o = pen_s, key_s, ow_f[0, 1]
    for r in range(n_rep):
        pen_o = jnp.maximum(pen_o, ow_f[r, 0])
        key_o = jnp.maximum(key_o, encode(ow_i[r, 0], ow_i[r, 1]))
        if r:
            gap_o = gap_o + ow_f[r, 1]
    none = pen_o < LOWEST_FILL * 0.5
    out_pen[...] = jnp.where(none, 0.0, pen_o)
    out_face[...] = jnp.where(none, -1, FACE_MASK - (key_o & FACE_MASK))
    out_gap[...] = gap_o + gap_s

    def end_tot(j, carry):
        tot_dom(j).wait_send()
        return carry

    lax.fori_loop(1, n_dom, end_tot, 0)
    for j in range(1, n_rep):
        rep_tot(j, rep).wait_send()
        for copy in own_copy(j, rep):
            copy.wait_send()
    for j in range(n_rep):
        for copy in spill_copy(j, rep):
            copy.wait_send()


def solution(mesh):
    n_dom, n_rep = mesh.shape["dom"], mesh.shape["rep"]

    def shards(ns, nm, sec, mst, off, qw, jac, slot, face, rank, live):
        k_size, p_size = ns.shape
        rows = sec.shape[1]
        lines = rows // LANES
        block = 1024
        b_lines = block // LANES
        grid = rows // block

        def lined(x):
            return x.reshape(lines, LANES)

        qrow = qw.reshape(1, p_size)
        off, jac, slot, face, rank = (lined(x) for x in (off, jac, slot, face, rank))
        smem = pl.BlockSpec(memory_space=pltpu.SMEM)
        full = lambda shape: pl.BlockSpec(shape, lambda i: (0, 0))
        line_spec = pl.BlockSpec((b_lines, LANES), lambda i: (i, 0))
        wide = pl.BlockSpec((k_size, block), lambda i: (0, i))
        force, pen, seg = pl.pallas_call(
            dense_kernel,
            grid=(grid,),
            out_shape=(
                jax.ShapeDtypeStruct((k_size, rows), jnp.bfloat16),
                jax.ShapeDtypeStruct((lines, LANES), jnp.float32),
                jax.ShapeDtypeStruct((PAD_GROUPS, LANES), jnp.float32),
            ),
            in_specs=[
                smem, full((k_size, p_size)), full((k_size, p_size)), full((1, p_size)),
                wide, wide, line_spec, line_spec, line_spec,
            ],
            out_specs=(wide, line_spec, full((PAD_GROUPS, LANES))),
            scratch_shapes=[
                pltpu.VMEM((p_size + 16, 2 * k_size), jnp.bfloat16),
                pltpu.VMEM((p_size, LANES), jnp.float32),
                pltpu.VMEM((SUB, LANES), jnp.float32),
            ],
            compiler_params=pltpu.CompilerParams(dimension_semantics=("arbitrary",)),
        )(live, ns, nm, qrow, sec, mst, off, jac, slot)

        vmem = pl.BlockSpec(memory_space=pltpu.VMEM)
        tile_f = (2, SUB, LANES)
        sems = pltpu.SemaphoreType.DMA
        seg_pen, seg_face, seg_gap, mean = pl.pallas_call(
            functools.partial(merge_kernel, n_dom, n_rep),
            out_shape=(
                jax.ShapeDtypeStruct((SUB, LANES), jnp.float32),
                jax.ShapeDtypeStruct((SUB, LANES), jnp.int32),
                jax.ShapeDtypeStruct((SUB, LANES), jnp.float32),
                jax.ShapeDtypeStruct((1,), jnp.float32),
            ),
            in_specs=[smem] + [vmem] * 7,
            out_specs=(vmem, vmem, vmem, smem),
            scratch_shapes=[
                pltpu.VMEM((GROUPS * lines + SUB, LANES), jnp.float32),
                pltpu.VMEM((GROUPS * lines + SUB, LANES), jnp.int32),
                pltpu.VMEM((GROUPS * LANES, LANES), jnp.float32),
                pltpu.VMEM((GROUPS * LANES, LANES), jnp.int32),
                pltpu.VMEM((n_rep,) + tile_f, jnp.float32),
                pltpu.VMEM((n_rep,) + tile_f, jnp.int32),
                pltpu.VMEM((n_rep,) + tile_f, jnp.float32),
                pltpu.VMEM((n_rep,) + tile_f, jnp.int32),
                pltpu.VMEM((n_dom, SUB, LANES), jnp.float32),
                pltpu.VMEM((n_rep, SUB, LANES), jnp.float32),
                pltpu.VMEM((SUB, LANES), jnp.float32),
                pltpu.VMEM(tile_f, jnp.float32),
                pltpu.VMEM(tile_f, jnp.int32),
                pltpu.VMEM((SUB, LANES), jnp.float32),
                pltpu.VMEM(tile_f, jnp.float32),
                pltpu.VMEM(tile_f, jnp.int32),
                pltpu.VMEM((SUB, LANES), jnp.float32),
                sems((n_rep,)), sems((n_rep,)), sems((n_rep,)), sems((n_rep,)),
                sems((n_rep,)), sems((n_rep,)), sems((n_rep,)), sems((n_rep,)),
                sems((n_dom,)), sems((n_dom,)), sems((n_rep,)), sems((n_rep,)),
            ],
            compiler_params=pltpu.CompilerParams(collective_id=0, has_side_effects=True),
        )(live, qrow, slot, face, rank, pen, jac, seg)
        return (
            force,
            seg_pen.reshape(SEG_DEV),
            seg_face.reshape(SEG_DEV),
            seg_gap.reshape(SEG_DEV),
            mean.reshape(()),
        )

    return jax.shard_map(
        shards,
        mesh=mesh,
        in_specs=(
            P(),
            P(),
            P(None, ("dom", "rep")),
            P(None, ("dom", "rep")),
            P(("dom", "rep")),
            P(),
            P(("dom", "rep")),
            P(("dom", "rep")),
            P(("dom", "rep")),
            P(("dom", "rep")),
            P(("dom", "rep")),
        ),
        out_specs=(P(None, ("dom", "rep")), P("dom"), P("dom"), P("dom"), P()),
        check_vma=False,
    )
```

time: 164 us -> 38.2 us (0.23)
  blocking collectives: 48.1 us -> 0 us
  other arithmetic: 42.5 us -> 0 us
  matrix products: 41.6 us -> 0 us
  Pallas kernels: 0 us -> 32.2 us
  local copies, waits for them, and re-layouts: 15.3 us -> 2.61 us
  starting transfers between devices: 7.87 us -> 0 us
  between operations: 6.72 us -> 3.06 us
    dot_general x12 -> x0, matrix products: 41.6 us -> none  [the longest x8 20.4 us: one_block(): lax.dot_general(take(paired), hit.astype(jnp.float32), (((1,), (1,)), (()...]
    pallas_call x0 -> x2, Pallas kernels: none -> 32.2 us  [the longest x1 21.1 us: shards(): pl.pallas_call(functools.partial(merge_kernel, n_dom, n_rep), out_shape=(...]
    all_gather x5 -> x0, blocking collectives: 27.3 us -> none  [combined_all(): pieces = jax.tree.map(lambda part: lax.all_gather(part, axis), value)]
    reduce_max x24 -> x0, other arithmetic: 25.4 us -> none  [the longest x8 10.2 us: one_block(): best_rank = jnp.max(jnp.where(hit, block_ranks[None, :], -1), axis=1)]
    psum x1 -> x0, blocking collectives: 20.8 us -> none  [shards(): gap_total, area_total = lax.psum((jnp.sum(own[3]), jnp.sum(own[4])), 'dom')]
    dynamic_slice x41 -> x0, local copies, waits for them, and re-layouts: 11.5 us -> none  [the longest x32 11.2 us: take(): return lax.dynamic_slice_in_dim(values, begin, block_len, values.ndim - 1)]
    ppermute x5 -> x0, starting transfers between devices: 7.87 us -> none  [passed_along(): lax.ppermute(x, axis, [(i, (i + by) % length) for i in range(length)])]
    select_n x23 -> x0, other arithmetic: 7.05 us -> none  [the longest x8 5.73 us: one_block(): jnp.where(block_live & (block_ranks == row_best), take(faces), FACE_LIMIT)]
  transfers between devices with their start and end apart: 5 -> 0, of which waited for: 0 -> 0; matrix products, arithmetic and copies ran while one was open for 6% -> 0% of each run, Pallas kernels for 0% -> 0%
where the time goes in v1:
time: 38.2 us; the launch traced here: 37.9 us
  Pallas kernels  32.2 us (84%)
  between operations  3.06 us (8%)
  local copies, waits for them, and re-layouts  2.61 us (7%)
    pallas_call x1, Pallas kernels, shards(): pl.pallas_call(functools.partial(merge_kernel, n_dom, n_rep), out_shape=(...  21.1 us
    pallas_call x1, Pallas kernels, shards(): pl.pallas_call(dense_kernel, grid=(grid,), out_shape=(jax.ShapeDtypeStruc...  11.1 us
    unnamed x9, local copies, waits for them, and re-layouts  2.61 us

profile of v1, /device:TPU:0, one launch (start us, length us, event | category | flops | bytes accessed | tf_op | source)
XLA Modules:
  0.0 37.9 jit_solution(14137723168836626727)
XLA Ops:
  1.3 11.1 %shard_map.146 = (bf16[64,8192]{1,0:T(8,128)(2,1)}, f32[64,128]{1,0:T(8,128)}, f32[16,128]{1,0:T(8,128)}) custom-call(s32[1]{0:T(128)S(6)} %copy.20.live_ref, bf16[64,256]{1,0:T(8,128)(2,1)} %ns_ref.1, bf16[64,256]{1,0:T(8,128)(2,1)} %nm_ref.1, f32[1,256]{1,0:T(1,128)} %bitcast.17, bf16[64,8192]{1,0:T(8,128)(2,1)} %sec_ref.1, bf16[64,8192]{1,0:T(8,128)(2,1)} %mst_ref.1, ...), custom_call_target="tpu_custom_call" | custom-call | tf_op jit(solution)/shard_map/pallas_call | solution.py:401
  12.4 21.1 %shard_map.147 = (f32[8,128]{1,0:T(8,128)}, s32[8,128]{1,0:T(8,128)}, f32[8,128]{1,0:T(8,128)}, f32[1]{0:T(128)}) custom-call(s32[1]{0:T(128)S(6)} %copy.20.live_ref, f32[1,256]{1,0:T(1,128)} %bitcast.18, s32[64,128]{1,0:T(8,128)} %bitcast.13, s32[64,128]{1,0:T(8,128)} %bitcast.15, s32[64,128]{1,0:T(8,128)} %bitcast.16, ...), custom_call_target="tpu_custom_call" | custom-call | tf_op jit(solution)/shard_map/pallas_call | solution.py:425
  33.5 0.0 copy-start.2
  33.5 0.7 %copy-done.2 = f32[8,128]{1,0:T(8,128)S(1)} copy-done((f32[8,128]{1,0:T(8,128)S(1)}, f32[8,128]{1,0:T(8,128)}, u32[]{:S(2)}) %copy-start.2) | copy-done | bytes 4120
  34.2 0.0 copy-start.1
  34.2 0.6 %copy.21 = f32[1024]{0:T(1024)} copy(f32[1024]{0:T(1024)S(1)} %bitcast.21) | data formatting | bytes 8192
  34.8 0.1 copy-done.1
  34.9 0.0 copy-start
  34.9 0.6 %copy.22 = s32[1024]{0:T(1024)} copy(s32[1024]{0:T(1024)S(1)} %bitcast.20) | data formatting | bytes 8192
  35.5 0.1 copy-done
  35.5 0.6 %copy.23 = f32[1024]{0:T(1024)} copy(f32[1024]{0:T(1024)S(1)} %bitcast.19) | data formatting | bytes 8192
Async XLA Ops:
  33.5 0.7 %copy-start.2 = (f32[8,128]{1,0:T(8,128)S(1)}, f32[8,128]{1,0:T(8,128)}, u32[]{:S(2)}) copy-start(f32[8,128]{1,0:T(8,128)} %get-tuple-element.15) | copy-start | bytes 12292
  34.2 0.7 %copy-start.1 = (s32[8,128]{1,0:T(8,128)S(1)}, s32[8,128]{1,0:T(8,128)}, u32[]{:S(2)}) copy-start(s32[8,128]{1,0:T(8,128)} %get-tuple-element.16) | copy-start | bytes 12292
  34.9 0.7 %copy-start = (f32[8,128]{1,0:T(8,128)S(1)}, f32[8,128]{1,0:T(8,128)}, u32[]{:S(2)}) copy-start(f32[8,128]{1,0:T(8,128)} %get-tuple-element.17) | copy-start | bytes 12292

commit v2 on v1

--- a/solution.py
+++ b/solution.py
@@ -22,6 +22,7 @@
 KEY_LOW = -2147483648
 MESH = pl.DeviceIdType.MESH
 TILE = 256
+DEPTH = 16
 
 
 def split3(x):
@@ -32,12 +33,67 @@
     return a, b, c
 
 
+def scan_group(g, depth0, code_ref, slot_ref, pen_ref, key_ref, packs, accs_pen, accs_key):
+    all_lines = code_ref.shape[0]
+    lane_lo, lane_pen, lane_key = packs
+    blocks = DEPTH // SUB
+    sub = lax.broadcasted_iota(jnp.int32, (SUB, LANES), 0)
+    wants = [(sub + (depth0 + SUB * b)) * PAD_GROUPS + g for b in range(blocks)]
+
+    def pull(i, carry):
+        los, pens, keys = (list(part) for part in carry)
+        code = code_ref[pl.ds(i, SUB, stride=0), :]
+        slot = slot_ref[pl.ds(i, SUB, stride=0), :]
+        pen = pen_ref[pl.ds(i, SUB, stride=0), :]
+        key = key_ref[pl.ds(i, SUB, stride=0), :]
+        for b in range(blocks):
+            hit = code == wants[b]
+            los[b] = jnp.where(hit, slot, los[b])
+            pens[b] = jnp.where(hit, pen, pens[b])
+            keys[b] = jnp.where(hit, key, keys[b])
+        return tuple(los), tuple(pens), tuple(keys)
+
+    none = jnp.full((SUB, LANES), -1, jnp.int32)
+    empty = jnp.full((SUB, LANES), LOWEST_FILL, jnp.float32)
+    start = ((none,) * blocks, (empty,) * blocks, (none,) * blocks)
+    los, pens, keys = lax.fori_loop(0, all_lines, pull, start, unroll=8)
+    for b in range(blocks):
+        rows = slice(SUB * b, SUB * (b + 1))
+        lane_lo[rows, :] = los[b]
+        lane_pen[rows, :] = pens[b]
+        lane_key[rows, :] = keys[b]
+
+    tiles = LANES // SUB
+    half = tiles // 2
+    for part in range(2):
+        marks = [sub + (g * LANES + SUB * (part * half + q)) for q in range(half)]
+        best_pen = [empty] * half
+        best_key = [jnp.full((SUB, LANES), KEY_LOW, jnp.int32)] * half
+        for j in range(DEPTH):
+            lo = lane_lo[pl.ds(j, SUB, stride=0), :]
+            pen = lane_pen[pl.ds(j, SUB, stride=0), :]
+            key = lane_key[pl.ds(j, SUB, stride=0), :]
+            for q in range(half):
+                hit = lo == marks[q]
+                best_pen[q] = jnp.maximum(best_pen[q], jnp.where(hit, pen, LOWEST_FILL))
+                best_key[q] = jnp.maximum(best_key[q], jnp.where(hit, key, KEY_LOW))
+        for q in range(half):
+            rows = slice(SUB * (part * half + q), SUB * (part * half + q + 1))
+            accs_pen[rows, :] = best_pen[q]
+            accs_key[rows, :] = best_key[q]
+    top = jnp.max(accs_pen[...].T, axis=0, keepdims=True)
+    best = jnp.max(accs_key[...].T, axis=0, keepdims=True)
+    return top, best
+
+
 def dense_kernel(
     live_ref, ns_ref, nm_ref, qw_ref, sec_ref, mst_ref, off_ref, jac_ref, slot_ref,
-    force_ref, pen_ref, seg_ref,
-    wt_ref, qcol_ref, qsum_ref,
+    face_ref, rank_ref,
+    force_ref, pen_ref, seg_ref, code_ref, key_ref, over_pen, over_key,
+    wt_ref, qcol_ref, qsum_ref, packs, accs_pen, accs_key,
 ):
     step = pl.program_id(0)
+    all_lines = slot_ref.shape[0]
     k_size, p_size = ns_ref.shape
     rows = sec_ref.shape[1]
     lines = rows // LANES
@@ -62,9 +118,33 @@
         wt_ref[p_size:, :] = stacked.astype(jnp.bfloat16)
         qsum_ref[...] = jnp.broadcast_to(jnp.sum(qmat, axis=0, keepdims=True), (SUB, LANES))
         seg_ref[...] = jnp.zeros_like(seg_ref)
+        over_pen[...] = jnp.full(over_pen.shape, LOWEST_FILL, jnp.float32)
+        over_key[...] = jnp.full(over_key.shape, KEY_LOW, jnp.int32)
+        row_id = (
+            lax.broadcasted_iota(jnp.int32, (all_lines, LANES), 0) * LANES
+            + lax.broadcasted_iota(jnp.int32, (all_lines, LANES), 1)
+        )
+        alive = row_id < live_ref[0]
+        key_ref[...] = ((rank_ref[...] - 2) << 30) + (FACE_MASK - face_ref[...])
+        group = jnp.where(alive, slot_ref[...] >> 7, -1)
+        before = (
+            lax.broadcasted_iota(jnp.int32, (all_lines, all_lines), 1)
+            < lax.broadcasted_iota(jnp.int32, (all_lines, all_lines), 0)
+        )
+        before = jnp.where(before, 1.0, 0.0).astype(jnp.bfloat16)
+        code = jnp.full((all_lines, LANES), -1, jnp.int32)
+        for g in range(GROUPS):
+            mine = group == g
+            place = jnp.dot(
+                before, jnp.where(mine, 1.0, 0.0).astype(jnp.bfloat16),
+                preferred_element_type=jnp.float32,
+            ).astype(jnp.int32)
+            code = jnp.where(mine, place * PAD_GROUPS + g, code)
+        code_ref[...] = code
 
     live_count = live_ref[0]
     first = step * rows
+    line0 = step * lines
     qcol = qcol_ref[...]
     qsum = qsum_ref[0:1, :]
     wt = wt_ref[...]
@@ -86,12 +166,12 @@
             jac_live = jnp.where(live, jac, 0.0)
             gap = field[:p_size, here] + offset
             lowest = jnp.min(gap, axis=0, keepdims=True)
-            pen_ref[line : line + 1, :] = jnp.where(live, -lowest, LOWEST_FILL)
+            pen_ref[pl.ds(line0 + line, 1), :] = jnp.where(live, -lowest, LOWEST_FILL)
             pieces.append((qcol * jnp.maximum(-gap, 0.0)).astype(jnp.bfloat16))
             scales.append(jac_live * PENALTY)
             summed = jnp.sum(field[p_size : p_size + SUB, here], axis=0, keepdims=True)
             row_gap = jac_live * (summed + offset * qsum)
-            slot = slot_ref[line : line + 1, :]
+            slot = slot_ref[pl.ds(line0 + line, 1), :]
             hi = slot >> 7
             lo = slot & (LANES - 1)
             hit_hi = lax.broadcasted_iota(jnp.int32, (PAD_GROUPS, LANES), 0) == hi
@@ -111,12 +191,37 @@
         force_ref[:, cols] = (force * jnp.concatenate(scales, axis=1)).astype(jnp.bfloat16)
     seg_ref[...] += seg_total
 
+    @pl.when(step == pl.num_programs(0) - 1)
+    def _():
+        code = code_ref[...]
+
+        @pl.when(jnp.max(code) >= DEPTH * PAD_GROUPS)
+        def _():
+            def one(g, carry):
+                for turn in range(1, all_lines // DEPTH):
+                    low = turn * DEPTH * PAD_GROUPS
+                    here = ((code & (PAD_GROUPS - 1)) == g) & (code >= low)
+                    found = jnp.max(jnp.where(here, 1.0, 0.0)) > 0.5
+
+                    @pl.when(found)
+                    def _():
+                        top, best = scan_group(
+                            g, turn * DEPTH, code_ref, slot_ref, pen_ref, key_ref,
+                            packs, accs_pen, accs_key,
+                        )
+                        at = pl.ds(g, 1)
+                        over_pen[at, :] = jnp.maximum(over_pen[at, :], top)
+                        over_key[at, :] = jnp.maximum(over_key[at, :], best)
+                return carry
+
+            lax.fori_loop(0, GROUPS, one, 0)
+
 
 def merge_kernel(
     n_dom, n_rep,
-    live_ref, qw_ref, slot_ref, face_ref, rank_ref, pen_ref, jac_ref, seg_ref,
-    out_pen, out_face, out_gap, out_mean,
-    pen_g, key_g, acc_pen, acc_key,
+    live_ref, qw_ref, slot_ref, code_ref, key_ref, pen_ref, jac_ref, seg_ref, over_pen, over_key,
+    out_pen, out_key, out_gap, out_mean,
+    lane_lo, lane_pen, lane_key, accs_pen, accs_key,
     sp_f, sp_i, ow_f, ow_i, tot_d, tot_r, tot_s,
     spill_f, spill_i, spill_t, own_f, own_i, own_t,
     s_spf, r_spf, s_spi, r_spi, s_owf, r_owf, s_owi, r_owi, s_td, r_td, s_tr, r_tr,
@@ -150,17 +255,6 @@
         + lax.broadcasted_iota(jnp.int32, (lines, LANES), 1)
     )
     live = row_id < live_count
-    slot = slot_ref[...]
-    hi = slot >> 7
-    key = jnp.where(
-        live, ((rank_ref[...] - 2) << 30) + (FACE_MASK - face_ref[...]), KEY_LOW
-    )
-    pen = pen_ref[...]
-    for g in range(GROUPS):
-        inside = hi == g
-        pen_g[g * lines : (g + 1) * lines, :] = jnp.where(inside, pen, LOWEST_FILL)
-        key_g[g * lines : (g + 1) * lines, :] = jnp.where(inside, key, KEY_LOW)
-
     total_gap = jnp.sum(jnp.sum(seg_ref[...], axis=0, keepdims=True), axis=1, keepdims=True)
     area_rows = jnp.where(live, jac_ref[...], 0.0)
     total_area = jnp.sum(
@@ -171,8 +265,6 @@
     tot_s[...] = pair
     tot_d[dom] = pair
 
-    pl.semaphore_wait(barrier, 3 * (n_rep - 1) + n_dom - 1)
-
     def tot_dom(j):
         return pltpu.make_async_remote_copy(
             src_ref=tot_s, dst_ref=tot_d.at[dom],
@@ -192,54 +284,13 @@
         tot_dom(j).start()
         return carry
 
-    lax.fori_loop(1, n_dom, start_tot, 0)
-
-    def scan_groups(g0, g1, per):
-        count = g1 - g0
-        width = SUB * per
-
-        def one(block, carry):
-            base = block * width
-            marks = [
-                lax.broadcasted_iota(jnp.int32, (SUB, LANES), 0) + (base + SUB * q)
-                for q in range(per)
-            ]
-
-            def body(i, accs):
-                accs = list(accs)
-                c = i
-                lo = slot_ref[pl.ds(c, SUB, stride=0), :] & (LANES - 1)
-                hits = [lo == m for m in marks]
-                for g in range(count):
-                    at = (g0 + g) * lines + c
-                    pv = pen_g[pl.ds(at, SUB, stride=0), :]
-                    kv = key_g[pl.ds(at, SUB, stride=0), :]
-                    for q in range(per):
-                        n = 2 * (g * per + q)
-                        accs[n] = jnp.maximum(accs[n], jnp.where(hits[q], pv, LOWEST_FILL))
-                        accs[n + 1] = jnp.maximum(accs[n + 1], jnp.where(hits[q], kv, KEY_LOW))
-                return tuple(accs)
-
-            start = (
-                jnp.full((SUB, LANES), LOWEST_FILL, jnp.float32),
-                jnp.full((SUB, LANES), KEY_LOW, jnp.int32),
-            ) * (count * per)
-            accs = lax.fori_loop(0, lines, body, start, unroll=4)
-            for g in range(count):
-                for q in range(per):
-                    n = 2 * (g * per + q)
-                    rows = pl.ds((g0 + g) * LANES + base + SUB * q, SUB)
-                    acc_pen[rows, :] = accs[n]
-                    acc_key[rows, :] = accs[n + 1]
-            return carry
-
-        lax.fori_loop(0, LANES // width, one, 0)
-
     def gather_group(g):
-        rows = pl.ds(g * LANES, LANES)
-        top = jnp.max(acc_pen[rows, :].T, axis=0, keepdims=True)
-        best = jnp.max(acc_key[rows, :].T, axis=0, keepdims=True)
-        return top, best
+        top, best = scan_group(
+            g, 0, code_ref, slot_ref, pen_ref, key_ref,
+            (lane_lo, lane_pen, lane_key), accs_pen, accs_key,
+        )
+        at = pl.ds(g, 1)
+        return jnp.maximum(top, over_pen[at, :]), jnp.maximum(best, over_key[at, :])
 
     def decode(top, best):
         none = top < LOWEST_FILL * 0.5
@@ -247,18 +298,24 @@
         face = jnp.where(none, FACE_LIMIT, FACE_MASK - (best & FACE_MASK))
         return rank, face
 
-    scan_groups(OWN_GROUPS, GROUPS, 4)
     spill_f[0] = jnp.full((SUB, LANES), LOWEST_FILL, jnp.float32)
     spill_i[0] = jnp.full((SUB, LANES), -1, jnp.int32)
     spill_i[1] = jnp.full((SUB, LANES), FACE_LIMIT, jnp.int32)
     spill_f[1] = seg_ref[OWN_GROUPS:, :]
-    for g in range(OWN_GROUPS, GROUPS):
+    def spill_group(g, carry):
         top, best = gather_group(g)
         rank, face = decode(top, best)
         at = pl.ds(g - OWN_GROUPS, 1)
         spill_f[0, at, :] = top
         spill_i[0, at, :] = rank
         spill_i[1, at, :] = face
+        return carry
+
+    lax.fori_loop(OWN_GROUPS, GROUPS, spill_group, 0)
+
+    pl.semaphore_wait(barrier, 3 * (n_rep - 1) + n_dom - 1)
+
+    lax.fori_loop(1, n_dom, start_tot, 0)
 
     def spill_copy(j, source):
         return (
@@ -278,38 +335,18 @@
         for copy in spill_copy(j, rep):
             copy.start()
 
-    def wait_tot(j, carry):
-        tot_dom_in(j).wait_recv()
-        return carry
-
-    lax.fori_loop(1, n_dom, wait_tot, 0)
-
-    def add_tot(j, total):
-        return total + tot_d[j]
-
-    dom_total = lax.fori_loop(0, n_dom, add_tot, jnp.zeros((SUB, LANES), jnp.float32))
-    own_t[...] = dom_total
-    tot_r[rep] = dom_total
-
-    def rep_tot(j, source):
-        return pltpu.make_async_remote_copy(
-            src_ref=own_t, dst_ref=tot_r.at[source],
-            send_sem=s_tr.at[j], recv_sem=r_tr.at[source],
-            device_id=dev(dom, rep + j), device_id_type=MESH,
-        )
-
-    for j in range(1, n_rep):
-        rep_tot(j, rep).start()
-
-    scan_groups(0, OWN_GROUPS, 2)
     own_f[1] = seg_ref[:OWN_GROUPS, :]
-    for g in range(OWN_GROUPS):
+
+    def own_group(g, carry):
         top, best = gather_group(g)
         rank, face = decode(top, best)
         at = pl.ds(g, 1)
         own_f[0, at, :] = top
         own_i[0, at, :] = rank
         own_i[1, at, :] = face
+        return carry
+
+    lax.fori_loop(0, OWN_GROUPS, own_group, 0)
 
     def own_copy(j, source):
         return (
@@ -330,6 +367,29 @@
             copy.start()
     ow_f[rep] = own_f[...]
     ow_i[rep] = own_i[...]
+
+    def wait_tot(j, carry):
+        tot_dom_in(j).wait_recv()
+        return carry
+
+    lax.fori_loop(1, n_dom, wait_tot, 0)
+
+    def add_tot(j, total):
+        return total + tot_d[j]
+
+    dom_total = lax.fori_loop(0, n_dom, add_tot, jnp.zeros((SUB, LANES), jnp.float32))
+    own_t[...] = dom_total
+    tot_r[rep] = dom_total
+
+    def rep_tot(j, source):
+        return pltpu.make_async_remote_copy(
+            src_ref=own_t, dst_ref=tot_r.at[source],
+            send_sem=s_tr.at[j], recv_sem=r_tr.at[source],
+            device_id=dev(dom, rep + j), device_id_type=MESH,
+        )
+
+    for j in range(1, n_rep):
+        rep_tot(j, rep).start()
 
     def encode(rank, face):
         return jnp.where(rank < 0, KEY_LOW, ((rank - 2) << 30) + (FACE_MASK - face))
@@ -359,9 +419,8 @@
         key_o = jnp.maximum(key_o, encode(ow_i[r, 0], ow_i[r, 1]))
         if r:
             gap_o = gap_o + ow_f[r, 1]
-    none = pen_o < LOWEST_FILL * 0.5
-    out_pen[...] = jnp.where(none, 0.0, pen_o)
-    out_face[...] = jnp.where(none, -1, FACE_MASK - (key_o & FACE_MASK))
+    out_pen[...] = pen_o
+    out_key[...] = key_o
     out_gap[...] = gap_o + gap_s
 
     def end_tot(j, carry):
@@ -398,31 +457,48 @@
         full = lambda shape: pl.BlockSpec(shape, lambda i: (0, 0))
         line_spec = pl.BlockSpec((b_lines, LANES), lambda i: (i, 0))
         wide = pl.BlockSpec((k_size, block), lambda i: (0, i))
-        force, pen, seg = pl.pallas_call(
+        whole = full((lines, LANES))
+        padded = full((PAD_GROUPS, LANES))
+        lane_packs = [
+            pltpu.VMEM((DEPTH + SUB, LANES), jnp.int32),
+            pltpu.VMEM((DEPTH + SUB, LANES), jnp.float32),
+            pltpu.VMEM((DEPTH + SUB, LANES), jnp.int32),
+        ]
+        lane_accs = [
+            pltpu.VMEM((LANES, LANES), jnp.float32),
+            pltpu.VMEM((LANES, LANES), jnp.int32),
+        ]
+        force, pen, seg, code, key, over_pen, over_key = pl.pallas_call(
             dense_kernel,
             grid=(grid,),
             out_shape=(
                 jax.ShapeDtypeStruct((k_size, rows), jnp.bfloat16),
                 jax.ShapeDtypeStruct((lines, LANES), jnp.float32),
                 jax.ShapeDtypeStruct((PAD_GROUPS, LANES), jnp.float32),
+                jax.ShapeDtypeStruct((lines, LANES), jnp.int32),
+                jax.ShapeDtypeStruct((lines, LANES), jnp.int32),
+                jax.ShapeDtypeStruct((PAD_GROUPS, LANES), jnp.float32),
+                jax.ShapeDtypeStruct((PAD_GROUPS, LANES), jnp.int32),
             ),
             in_specs=[
                 smem, full((k_size, p_size)), full((k_size, p_size)), full((1, p_size)),
-                wide, wide, line_spec, line_spec, line_spec,
+                wide, wide, line_spec, line_spec, whole, whole, whole,
             ],
-            out_specs=(wide, line_spec, full((PAD_GROUPS, LANES))),
+            out_specs=(wide, whole, padded, whole, whole, padded, padded),
             scratch_shapes=[
                 pltpu.VMEM((p_size + 16, 2 * k_size), jnp.bfloat16),
                 pltpu.VMEM((p_size, LANES), jnp.float32),
                 pltpu.VMEM((SUB, LANES), jnp.float32),
+                lane_packs,
+                *lane_accs,
             ],
             compiler_params=pltpu.CompilerParams(dimension_semantics=("arbitrary",)),
-        )(live, ns, nm, qrow, sec, mst, off, jac, slot)
+        )(live, ns, nm, qrow, sec, mst, off, jac, slot, face, rank)
 
         vmem = pl.BlockSpec(memory_space=pltpu.VMEM)
         tile_f = (2, SUB, LANES)
         sems = pltpu.SemaphoreType.DMA
-        seg_pen, seg_face, seg_gap, mean = pl.pallas_call(
+        best_pen, best_key, gap_sum, mean = pl.pallas_call(
             functools.partial(merge_kernel, n_dom, n_rep),
             out_shape=(
                 jax.ShapeDtypeStruct((SUB, LANES), jnp.float32),
@@ -430,13 +506,11 @@
                 jax.ShapeDtypeStruct((SUB, LANES), jnp.float32),
                 jax.ShapeDtypeStruct((1,), jnp.float32),
             ),
-            in_specs=[smem] + [vmem] * 7,
+            in_specs=[smem] + [vmem] * 9,
             out_specs=(vmem, vmem, vmem, smem),
             scratch_shapes=[
-                pltpu.VMEM((GROUPS * lines + SUB, LANES), jnp.float32),
-                pltpu.VMEM((GROUPS * lines + SUB, LANES), jnp.int32),
-                pltpu.VMEM((GROUPS * LANES, LANES), jnp.float32),
-                pltpu.VMEM((GROUPS * LANES, LANES), jnp.int32),
+                *lane_packs,
+                *lane_accs,
                 pltpu.VMEM((n_rep,) + tile_f, jnp.float32),
                 pltpu.VMEM((n_rep,) + tile_f, jnp.int32),
                 pltpu.VMEM((n_rep,) + tile_f, jnp.float32),
@@ -455,14 +529,13 @@
                 sems((n_dom,)), sems((n_dom,)), sems((n_rep,)), sems((n_rep,)),
             ],
             compiler_params=pltpu.CompilerParams(collective_id=0, has_side_effects=True),
-        )(live, qrow, slot, face, rank, pen, jac, seg)
-        return (
-            force,
-            seg_pen.reshape(SEG_DEV),
-            seg_face.reshape(SEG_DEV),
-            seg_gap.reshape(SEG_DEV),
-            mean.reshape(()),
-        )
+        )(live, qrow, slot, code, key, pen, jac, seg, over_pen, over_key)
+        best_pen, best_key, gap_sum = (x.reshape(SEG_DEV) for x in (best_pen, best_key, gap_sum))
+        none = best_pen < LOWEST_FILL * 0.5
+        seg_pen = jnp.where(none, 0.0, best_pen)
+        seg_face = jnp.where(none, -1, FACE_MASK - (best_key & FACE_MASK))
+        seg_gap = jnp.where(none, 0.0, gap_sum)
+        return force, seg_pen, seg_face, seg_gap, mean.reshape(())
 
     return jax.shard_map(
         shards,

time: 38.2 us -> 31.4 us (0.82)
  Pallas kernels: 32.2 us -> 26.2 us
  local copies, waits for them, and re-layouts: 2.61 us -> 0.76 us
  other arithmetic: 0 us -> 1.2 us
    pallas_call x1, Pallas kernels: 21.1 us -> 14.7 us  [shards(): pl.pallas_call(functools.partial(merge_kernel, n_dom, n_rep), out_shape=(...]
    unnamed x9 -> x6, local copies, waits for them, and re-layouts: 2.61 us -> 0.76 us
    select_n x0 -> x2, other arithmetic: none -> 1.2 us  [the longest x1 0.6 us: shards(): seg_gap = jnp.where(none, 0.0, gap_sum)]
where the time goes in v2:
time: 31.4 us; the launch traced here: 31.1 us
  Pallas kernels  26.2 us (83%)
  between operations  2.99 us (10%)
  other arithmetic  1.2 us (4%)
  local copies, waits for them, and re-layouts  0.76 us (2%)
    pallas_call x1, Pallas kernels, shards(): pl.pallas_call(functools.partial(merge_kernel, n_dom, n_rep), out_shape=(...  14.7 us
    pallas_call x1, Pallas kernels, shards(): pl.pallas_call(dense_kernel, grid=(grid,), out_shape=(jax.ShapeDtypeStruc...  11.5 us
    unnamed x6, local copies, waits for them, and re-layouts  0.76 us

profile of v2, /device:TPU:0, one launch (start us, length us, event | category | flops | bytes accessed | tf_op | source)
XLA Modules:
  0.0 31.1 jit_solution(5479478716753444691)
XLA Ops:
  1.3 11.5 %shard_map.146 = (bf16[64,8192]{1,0:T(8,128)(2,1)}, f32[64,128]{1,0:T(8,128)}, f32[16,128]{1,0:T(8,128)}, s32[64,128]{1,0:T(8,128)}, s32[64,128]{1,0:T(8,128)}, /*index=5*/f32[16,128]{1,0:T(8,128)}, s32[16,128]{1,0:T(8,128)}) custom-call(s32[1]{0:T(128)S(6)} %copy.17.live_ref, bf16[64,256]{1,0:T(8,128)(2,1)} %ns_ref.1, bf16[64,256]{1,0:T(8,128)(2,1)} %nm_ref.1, ...), custom_call_target="tpu_custom_call" | custom-call | tf_op jit(solution)/shard_map/pallas_call | solution.py:471
  12.7 14.7 %shard_map.147 = (f32[8,128]{1,0:T(8,128)}, s32[8,128]{1,0:T(8,128)}, f32[8,128]{1,0:T(8,128)}, f32[1]{0:T(128)}) custom-call(s32[1]{0:T(128)S(6)} %copy.17.live_ref, f32[1,256]{1,0:T(1,128)} %bitcast.28, s32[64,128]{1,0:T(8,128)} %bitcast.23, s32[64,128]{1,0:T(8,128)} %get-tuple-element.17.code_ref, s32[64,128]{1,0:T(8,128)} %get-tuple-element.18.key_ref, ...), custom_call_target="tpu_custom_call" | custom-call | tf_op jit(solution)/shard_map/pallas_call | solution.py:501
  27.5 0.0 copy-start.1
  27.5 0.0 copy-start
  27.5 0.7 %copy-done.1 = s32[8,128]{1,0:T(8,128)S(1)} copy-done((s32[8,128]{1,0:T(8,128)S(1)}, s32[8,128]{1,0:T(8,128)}, u32[]{:S(2)}) %copy-start.1) | copy-done | bytes 4120
  28.2 0.0 copy-done
  28.2 0.0 copy-start.2
  28.2 0.6 %bitcast_select_fusion.1 = s32[1024]{0:T(1024)} fusion(s32[8,128]{1,0:T(8,128)S(1)} %copy-done.1, f32[8,128]{1,0:T(8,128)S(1)} %copy-done), kind=kLoop, calls=%fused_computation.1 | loop fusion | flops 4096 | bytes 12288 | tf_op jit(solution)/shard_map/jit(_where)/select_n | solution.py:536
  28.8 0.1 copy-done.2
  28.9 0.6 %bitcast_select_fusion = (f32[1024]{0:T(1024)}, f32[1024]{0:T(1024)}) fusion(f32[8,128]{1,0:T(8,128)S(1)} %copy-done.2, f32[8,128]{1,0:T(8,128)S(1)} %copy-done), kind=kLoop, calls=%fused_computation | loop fusion | flops 3072 | bytes 16384 | tf_op jit(solution)/shard_map/jit(_where)/select_n | solution.py:537
Async XLA Ops:
  27.5 0.7 %copy-start.1 = (s32[8,128]{1,0:T(8,128)S(1)}, s32[8,128]{1,0:T(8,128)}, u32[]{:S(2)}) copy-start(s32[8,128]{1,0:T(8,128)} %get-tuple-element.24) | copy-start | bytes 12292
  27.5 0.7 %copy-start = (f32[8,128]{1,0:T(8,128)S(1)}, f32[8,128]{1,0:T(8,128)}, u32[]{:S(2)}) copy-start(f32[8,128]{1,0:T(8,128)} %get-tuple-element.23) | copy-start | bytes 12292
  28.2 0.7 %copy-start.2 = (f32[8,128]{1,0:T(8,128)S(1)}, f32[8,128]{1,0:T(8,128)}, u32[]{:S(2)}) copy-start(f32[8,128]{1,0:T(8,128)} %get-tuple-element.25) | copy-start | bytes 12292

commit v3 on v2

--- a/solution.py
+++ b/solution.py
@@ -23,6 +23,7 @@
 MESH = pl.DeviceIdType.MESH
 TILE = 256
 DEPTH = 16
+BLOCK = 1024
 
 
 def split3(x):
@@ -33,10 +34,10 @@
     return a, b, c
 
 
-def scan_group(g, depth0, code_ref, slot_ref, pen_ref, key_ref, packs, accs_pen, accs_key):
+def scan_group(g, depth0, depth, code_ref, slot_ref, pen_ref, key_ref, packs, accs_pen, accs_key):
     all_lines = code_ref.shape[0]
     lane_lo, lane_pen, lane_key = packs
-    blocks = DEPTH // SUB
+    blocks = depth // SUB
     sub = lax.broadcasted_iota(jnp.int32, (SUB, LANES), 0)
     wants = [(sub + (depth0 + SUB * b)) * PAD_GROUPS + g for b in range(blocks)]
 
@@ -69,7 +70,7 @@
         marks = [sub + (g * LANES + SUB * (part * half + q)) for q in range(half)]
         best_pen = [empty] * half
         best_key = [jnp.full((SUB, LANES), KEY_LOW, jnp.int32)] * half
-        for j in range(DEPTH):
+        for j in range(depth):
             lo = lane_lo[pl.ds(j, SUB, stride=0), :]
             pen = lane_pen[pl.ds(j, SUB, stride=0), :]
             key = lane_key[pl.ds(j, SUB, stride=0), :]
@@ -193,28 +194,22 @@
 
     @pl.when(step == pl.num_programs(0) - 1)
     def _():
-        code = code_ref[...]
-
-        @pl.when(jnp.max(code) >= DEPTH * PAD_GROUPS)
-        def _():
-            def one(g, carry):
-                for turn in range(1, all_lines // DEPTH):
-                    low = turn * DEPTH * PAD_GROUPS
-                    here = ((code & (PAD_GROUPS - 1)) == g) & (code >= low)
-                    found = jnp.max(jnp.where(here, 1.0, 0.0)) > 0.5
-
-                    @pl.when(found)
-                    def _():
-                        top, best = scan_group(
-                            g, turn * DEPTH, code_ref, slot_ref, pen_ref, key_ref,
-                            packs, accs_pen, accs_key,
-                        )
-                        at = pl.ds(g, 1)
-                        over_pen[at, :] = jnp.maximum(over_pen[at, :], top)
-                        over_key[at, :] = jnp.maximum(over_key[at, :], best)
-                return carry
-
-            lax.fori_loop(0, GROUPS, one, 0)
+        def one(worst):
+            code = code_ref[...]
+            g = worst & (PAD_GROUPS - 1)
+            low = (worst >> 4) & -SUB
+            top, best = scan_group(
+                g, low, SUB, code_ref, slot_ref, pen_ref, key_ref, packs, accs_pen, accs_key
+            )
+            at = pl.ds(g, 1)
+            over_pen[at, :] = jnp.maximum(over_pen[at, :], top)
+            over_key[at, :] = jnp.maximum(over_key[at, :], best)
+            done = ((code & (PAD_GROUPS - 1)) == g) & (code >= low * PAD_GROUPS)
+            code = jnp.where(done, -1, code)
+            code_ref[...] = code
+            return jnp.max(code)
+
+        lax.while_loop(lambda worst: worst >= DEPTH * PAD_GROUPS, one, jnp.max(code_ref[...]))
 
 
 def merge_kernel(
@@ -286,7 +281,7 @@
 
     def gather_group(g):
         top, best = scan_group(
-            g, 0, code_ref, slot_ref, pen_ref, key_ref,
+            g, 0, DEPTH, code_ref, slot_ref, pen_ref, key_ref,
             (lane_lo, lane_pen, lane_key), accs_pen, accs_key,
         )
         at = pl.ds(g, 1)
@@ -437,6 +432,60 @@
             copy.wait_send()
 
 
+def lane_scratch():
+    lane_packs = [
+        pltpu.VMEM((DEPTH + SUB, LANES), jnp.int32),
+        pltpu.VMEM((DEPTH + SUB, LANES), jnp.float32),
+        pltpu.VMEM((DEPTH + SUB, LANES), jnp.int32),
+    ]
+    lane_accs = [
+        pltpu.VMEM((LANES, LANES), jnp.float32),
+        pltpu.VMEM((LANES, LANES), jnp.int32),
+    ]
+    return lane_packs, lane_accs
+
+
+def dense_call(live, ns, nm, qrow, sec, mst, off, jac, slot, face, rank, block=BLOCK):
+    k_size, p_size = ns.shape
+    rows = sec.shape[1]
+    lines = rows // LANES
+    b_lines = block // LANES
+    grid = rows // block
+    smem = pl.BlockSpec(memory_space=pltpu.SMEM)
+    full = lambda shape: pl.BlockSpec(shape, lambda i: (0, 0))
+    line_spec = pl.BlockSpec((b_lines, LANES), lambda i: (i, 0))
+    wide = pl.BlockSpec((k_size, block), lambda i: (0, i))
+    whole = full((lines, LANES))
+    padded = full((PAD_GROUPS, LANES))
+    lane_packs, lane_accs = lane_scratch()
+    return pl.pallas_call(
+        dense_kernel,
+        grid=(grid,),
+        out_shape=(
+            jax.ShapeDtypeStruct((k_size, rows), jnp.bfloat16),
+            jax.ShapeDtypeStruct((lines, LANES), jnp.float32),
+            jax.ShapeDtypeStruct((PAD_GROUPS, LANES), jnp.float32),
+            jax.ShapeDtypeStruct((lines, LANES), jnp.int32),
+            jax.ShapeDtypeStruct((lines, LANES), jnp.int32),
+            jax.ShapeDtypeStruct((PAD_GROUPS, LANES), jnp.float32),
+            jax.ShapeDtypeStruct((PAD_GROUPS, LANES), jnp.int32),
+        ),
+        in_specs=[
+            smem, full((k_size, p_size)), full((k_size, p_size)), full((1, p_size)),
+            wide, wide, line_spec, line_spec, whole, whole, whole,
+        ],
+        out_specs=(wide, whole, padded, whole, whole, padded, padded),
+        scratch_shapes=[
+            pltpu.VMEM((p_size + 16, 2 * k_size), jnp.bfloat16),
+            pltpu.VMEM((p_size, LANES), jnp.float32),
+            pltpu.VMEM((SUB, LANES), jnp.float32),
+            lane_packs,
+            *lane_accs,
+        ],
+        compiler_params=pltpu.CompilerParams(dimension_semantics=("arbitrary",)),
+    )(live, ns, nm, qrow, sec, mst, off, jac, slot, face, rank)
+
+
 def solution(mesh):
     n_dom, n_rep = mesh.shape["dom"], mesh.shape["rep"]
 
@@ -444,9 +493,6 @@
         k_size, p_size = ns.shape
         rows = sec.shape[1]
         lines = rows // LANES
-        block = 1024
-        b_lines = block // LANES
-        grid = rows // block
 
         def lined(x):
             return x.reshape(lines, LANES)
@@ -454,46 +500,10 @@
         qrow = qw.reshape(1, p_size)
         off, jac, slot, face, rank = (lined(x) for x in (off, jac, slot, face, rank))
         smem = pl.BlockSpec(memory_space=pltpu.SMEM)
-        full = lambda shape: pl.BlockSpec(shape, lambda i: (0, 0))
-        line_spec = pl.BlockSpec((b_lines, LANES), lambda i: (i, 0))
-        wide = pl.BlockSpec((k_size, block), lambda i: (0, i))
-        whole = full((lines, LANES))
-        padded = full((PAD_GROUPS, LANES))
-        lane_packs = [
-            pltpu.VMEM((DEPTH + SUB, LANES), jnp.int32),
-            pltpu.VMEM((DEPTH + SUB, LANES), jnp.float32),
-            pltpu.VMEM((DEPTH + SUB, LANES), jnp.int32),
-        ]
-        lane_accs = [
-            pltpu.VMEM((LANES, LANES), jnp.float32),
-            pltpu.VMEM((LANES, LANES), jnp.int32),
-        ]
-        force, pen, seg, code, key, over_pen, over_key = pl.pallas_call(
-            dense_kernel,
-            grid=(grid,),
-            out_shape=(
-                jax.ShapeDtypeStruct((k_size, rows), jnp.bfloat16),
-                jax.ShapeDtypeStruct((lines, LANES), jnp.float32),
-                jax.ShapeDtypeStruct((PAD_GROUPS, LANES), jnp.float32),
-                jax.ShapeDtypeStruct((lines, LANES), jnp.int32),
-                jax.ShapeDtypeStruct((lines, LANES), jnp.int32),
-                jax.ShapeDtypeStruct((PAD_GROUPS, LANES), jnp.float32),
-                jax.ShapeDtypeStruct((PAD_GROUPS, LANES), jnp.int32),
-            ),
-            in_specs=[
-                smem, full((k_size, p_size)), full((k_size, p_size)), full((1, p_size)),
-                wide, wide, line_spec, line_spec, whole, whole, whole,
-            ],
-            out_specs=(wide, whole, padded, whole, whole, padded, padded),
-            scratch_shapes=[
-                pltpu.VMEM((p_size + 16, 2 * k_size), jnp.bfloat16),
-                pltpu.VMEM((p_size, LANES), jnp.float32),
-                pltpu.VMEM((SUB, LANES), jnp.float32),
-                lane_packs,
-                *lane_accs,
-            ],
-            compiler_params=pltpu.CompilerParams(dimension_semantics=("arbitrary",)),
-        )(live, ns, nm, qrow, sec, mst, off, jac, slot, face, rank)
+        lane_packs, lane_accs = lane_scratch()
+        force, pen, seg, code, key, over_pen, over_key = dense_call(
+            live, ns, nm, qrow, sec, mst, off, jac, slot, face, rank
+        )
 
         vmem = pl.BlockSpec(memory_space=pltpu.VMEM)
         tile_f = (2, SUB, LANES)

time: 31.4 us -> 31.4 us (level)
  no operation moved by 1% of the time
where the time goes in v3:
time: 31.4 us; the launch traced here: 31.1 us
  Pallas kernels  26.2 us (83%)
  between operations  2.99 us (10%)
  other arithmetic  1.2 us (4%)
  local copies, waits for them, and re-layouts  0.76 us (2%)
    pallas_call x1, Pallas kernels, shards(): pl.pallas_call(functools.partial(merge_kernel, n_dom, n_rep), out_shape=(...  14.7 us
    pallas_call x1, Pallas kernels, dense_call(): pl.pallas_call(dense_kernel, grid=(grid,), out_shape=(jax.ShapeDtypeStruc...  11.4 us
    unnamed x6, local copies, waits for them, and re-layouts  0.76 us

profile of v3, /device:TPU:0, one launch (start us, length us, event | category | flops | bytes accessed | tf_op | source)
XLA Modules:
  0.0 31.1 jit_solution(5060720190070537957)
XLA Ops:
  1.3 11.4 %shard_map.146 = (bf16[64,8192]{1,0:T(8,128)(2,1)}, f32[64,128]{1,0:T(8,128)}, f32[16,128]{1,0:T(8,128)}, s32[64,128]{1,0:T(8,128)}, s32[64,128]{1,0:T(8,128)}, /*index=5*/f32[16,128]{1,0:T(8,128)}, s32[16,128]{1,0:T(8,128)}) custom-call(s32[1]{0:T(128)S(6)} %copy.17.live_ref, bf16[64,256]{1,0:T(8,128)(2,1)} %ns_ref.1, bf16[64,256]{1,0:T(8,128)(2,1)} %nm_ref.1, ...), custom_call_target="tpu_custom_call" | custom-call | tf_op jit(solution)/shard_map/pallas_call | solution.py:461
  12.7 14.7 %shard_map.147 = (f32[8,128]{1,0:T(8,128)}, s32[8,128]{1,0:T(8,128)}, f32[8,128]{1,0:T(8,128)}, f32[1]{0:T(128)}) custom-call(s32[1]{0:T(128)S(6)} %copy.17.live_ref, f32[1,256]{1,0:T(1,128)} %bitcast.28, s32[64,128]{1,0:T(8,128)} %bitcast.23, s32[64,128]{1,0:T(8,128)} %get-tuple-element.17.code_ref, s32[64,128]{1,0:T(8,128)} %get-tuple-element.18.key_ref, ...), custom_call_target="tpu_custom_call" | custom-call | tf_op jit(solution)/shard_map/pallas_call | solution.py:511
  27.5 0.0 copy-start.1
  27.5 0.0 copy-start
  27.5 0.7 %copy-done.1 = s32[8,128]{1,0:T(8,128)S(1)} copy-done((s32[8,128]{1,0:T(8,128)S(1)}, s32[8,128]{1,0:T(8,128)}, u32[]{:S(2)}) %copy-start.1) | copy-done | bytes 4120
  28.2 0.0 copy-done
  28.2 0.0 copy-start.2
  28.2 0.6 %bitcast_select_fusion.1 = s32[1024]{0:T(1024)} fusion(s32[8,128]{1,0:T(8,128)S(1)} %copy-done.1, f32[8,128]{1,0:T(8,128)S(1)} %copy-done), kind=kLoop, calls=%fused_computation.1 | loop fusion | flops 4096 | bytes 12288 | tf_op jit(solution)/shard_map/jit(_where)/select_n | solution.py:546
  28.8 0.1 copy-done.2
  28.9 0.6 %bitcast_select_fusion = (f32[1024]{0:T(1024)}, f32[1024]{0:T(1024)}) fusion(f32[8,128]{1,0:T(8,128)S(1)} %copy-done.2, f32[8,128]{1,0:T(8,128)S(1)} %copy-done), kind=kLoop, calls=%fused_computation | loop fusion | flops 3072 | bytes 16384 | tf_op jit(solution)/shard_map/jit(_where)/select_n | solution.py:547
Async XLA Ops:
  27.5 0.7 %copy-start.1 = (s32[8,128]{1,0:T(8,128)S(1)}, s32[8,128]{1,0:T(8,128)}, u32[]{:S(2)}) copy-start(s32[8,128]{1,0:T(8,128)} %get-tuple-element.24) | copy-start | bytes 12292
  27.5 0.7 %copy-start = (f32[8,128]{1,0:T(8,128)S(1)}, f32[8,128]{1,0:T(8,128)}, u32[]{:S(2)}) copy-start(f32[8,128]{1,0:T(8,128)} %get-tuple-element.23) | copy-start | bytes 12292
  28.2 0.7 %copy-start.2 = (f32[8,128]{1,0:T(8,128)S(1)}, f32[8,128]{1,0:T(8,128)}, u32[]{:S(2)}) copy-start(f32[8,128]{1,0:T(8,128)} %get-tuple-element.25) | copy-start | bytes 12292

commit v4 on v3

--- a/solution.py
+++ b/solution.py
@@ -23,7 +23,7 @@
 MESH = pl.DeviceIdType.MESH
 TILE = 256
 DEPTH = 16
-BLOCK = 1024
+BLOCK = 2048
 
 
 def split3(x):
@@ -91,7 +91,7 @@
     live_ref, ns_ref, nm_ref, qw_ref, sec_ref, mst_ref, off_ref, jac_ref, slot_ref,
     face_ref, rank_ref,
     force_ref, pen_ref, seg_ref, code_ref, key_ref, over_pen, over_key,
-    wt_ref, qcol_ref, qsum_ref, packs, accs_pen, accs_key,
+    wt_ref, nq_ref, packs, accs_pen, accs_key,
 ):
     step = pl.program_id(0)
     all_lines = slot_ref.shape[0]
@@ -105,19 +105,25 @@
         w = jnp.concatenate([ns_ref[...], -nm_ref[...]], axis=0).astype(jnp.float32)
         qrow = qw_ref[...]
         wt = w.T
-        wt_ref[0:p_size, :] = wt.astype(jnp.bfloat16)
         qmat = jnp.broadcast_to(qrow, (LANES, p_size)).T
-        qcol_ref[...] = qmat
         v = jnp.sum(wt * qmat, axis=0, keepdims=True)
-        a, b, c = split3(v)
-        pick = lax.broadcasted_iota(jnp.int32, (16, 2 * k_size), 0)
+        qsum = jnp.sum(qmat, axis=0, keepdims=True)
+        depth = wt_ref.shape[1]
+        pick = lax.broadcasted_iota(jnp.int32, (16, depth), 0)
+        column = lax.broadcasted_iota(jnp.int32, (p_size, depth - 2 * k_size), 1)
+        wt_ref[0:p_size, 0 : 2 * k_size] = wt.astype(jnp.bfloat16)
+        wt_ref[0:p_size, 2 * k_size :] = jnp.where(column < 3, 1.0, 0.0).astype(jnp.bfloat16)
+        lane_row = lax.broadcasted_iota(jnp.int32, (1, LANES), 1)
+        tail = jnp.where(lane_row < 3, qsum, 0.0)[:, : depth - 2 * k_size]
+        a, b, c = (part.astype(jnp.float32) for part in split3(jnp.concatenate([v, tail], axis=1)))
         stacked = jnp.where(
-            pick == 0,
-            a.astype(jnp.float32),
-            jnp.where(pick == 1, b.astype(jnp.float32), jnp.where(pick == 2, c.astype(jnp.float32), 0.0)),
+            pick == 0, a, jnp.where(pick == 1, b, jnp.where(pick == 2, c, 0.0))
         )
         wt_ref[p_size:, :] = stacked.astype(jnp.bfloat16)
-        qsum_ref[...] = jnp.broadcast_to(jnp.sum(qmat, axis=0, keepdims=True), (SUB, LANES))
+        scaled = ns_ref[...].astype(jnp.float32) * qrow
+        top = scaled.astype(jnp.bfloat16)
+        low = (scaled - top.astype(jnp.float32)).astype(jnp.bfloat16)
+        nq_ref[...] = jnp.concatenate([top, low], axis=0)
         seg_ref[...] = jnp.zeros_like(seg_ref)
         over_pen[...] = jnp.full(over_pen.shape, LOWEST_FILL, jnp.float32)
         over_key[...] = jnp.full(over_key.shape, KEY_LOW, jnp.int32)
@@ -146,50 +152,54 @@
     live_count = live_ref[0]
     first = step * rows
     line0 = step * lines
-    qcol = qcol_ref[...]
-    qsum = qsum_ref[0:1, :]
     wt = wt_ref[...]
-    ns = ns_ref[...]
-    lane = lax.broadcasted_iota(jnp.int32, (1, LANES), 1)
+    nq = nq_ref[...]
     seg_total = jnp.zeros((PAD_GROUPS, LANES), jnp.float32)
-    for tile in range(rows // TILE):
+    pad_rows = wt.shape[1] - 2 * k_size
+    pad_id = lax.broadcasted_iota(jnp.int32, (pad_rows, TILE), 0)
+
+    def line_of(ref, at, count):
+        return jnp.concatenate([ref[pl.ds(at + i, 1), :] for i in range(count)], axis=1)
+
+    def project(tile):
         cols = pl.ds(tile * TILE, TILE)
-        x = jnp.concatenate([sec_ref[:, cols], mst_ref[:, cols]], axis=0)
-        field = jnp.dot(wt, x, preferred_element_type=jnp.float32)
-        pieces = []
-        scales = []
+        offset = line_of(off_ref, tile * per_tile, per_tile)
+        a, b, c = (part.astype(jnp.float32) for part in split3(offset))
+        extra = jnp.where(pad_id == 0, a, jnp.where(pad_id == 1, b, jnp.where(pad_id == 2, c, 0.0)))
+        x = jnp.concatenate([sec_ref[:, cols], mst_ref[:, cols], extra.astype(jnp.bfloat16)], axis=0)
+        return jnp.dot(wt, x, preferred_element_type=jnp.float32)
+
+    row_lane = lax.broadcasted_iota(jnp.int32, (1, TILE), 1)
+    hi_id = lax.broadcasted_iota(jnp.int32, (PAD_GROUPS, TILE), 0)
+    lo_id = lax.broadcasted_iota(jnp.int32, (LANES, TILE), 0)
+    tiles = rows // TILE
+    field = project(0)
+    for tile in range(tiles):
+        cols = pl.ds(tile * TILE, TILE)
+        coming = project(tile + 1) if tile + 1 < tiles else None
+        gap = field[:p_size]
+        live = (row_lane + (first + tile * TILE)) < live_count
+        jac_live = jnp.where(live, line_of(jac_ref, tile * per_tile, per_tile), 0.0)
+        load = jnp.minimum(gap.astype(jnp.bfloat16), 0)
+        force = jnp.dot(nq, load, preferred_element_type=jnp.float32)
+        force_ref[:, cols] = (
+            (force[:k_size] + force[k_size:]) * (jac_live * -PENALTY)
+        ).astype(jnp.bfloat16)
+        pen = jnp.where(live, -jnp.min(gap, axis=0, keepdims=True), LOWEST_FILL)
         for part in range(per_tile):
-            line = tile * per_tile + part
-            here = slice(part * LANES, (part + 1) * LANES)
-            offset = off_ref[line : line + 1, :]
-            live = (lane + (first + line * LANES)) < live_count
-            jac = jac_ref[line : line + 1, :]
-            jac_live = jnp.where(live, jac, 0.0)
-            gap = field[:p_size, here] + offset
-            lowest = jnp.min(gap, axis=0, keepdims=True)
-            pen_ref[pl.ds(line0 + line, 1), :] = jnp.where(live, -lowest, LOWEST_FILL)
-            pieces.append((qcol * jnp.maximum(-gap, 0.0)).astype(jnp.bfloat16))
-            scales.append(jac_live * PENALTY)
-            summed = jnp.sum(field[p_size : p_size + SUB, here], axis=0, keepdims=True)
-            row_gap = jac_live * (summed + offset * qsum)
-            slot = slot_ref[pl.ds(line0 + line, 1), :]
-            hi = slot >> 7
-            lo = slot & (LANES - 1)
-            hit_hi = lax.broadcasted_iota(jnp.int32, (PAD_GROUPS, LANES), 0) == hi
-            hit_lo = lax.broadcasted_iota(jnp.int32, (LANES, LANES), 0) == lo
-            spread = jnp.where(hit_hi, row_gap, 0.0)
-            a, b, c = split3(spread)
-            left = jnp.concatenate([a, b, c], axis=0)
-            right = jnp.where(hit_lo, 1.0, 0.0).astype(jnp.bfloat16)
-            got = lax.dot_general(
-                left, right, (((1,), (1,)), ((), ())), preferred_element_type=jnp.float32
-            )
-            seg_total = seg_total + (
-                got[0:PAD_GROUPS] + got[PAD_GROUPS : 2 * PAD_GROUPS] + got[2 * PAD_GROUPS :]
-            )
-        load = jnp.concatenate(pieces, axis=1)
-        force = jnp.dot(ns, load, preferred_element_type=jnp.float32)
-        force_ref[:, cols] = (force * jnp.concatenate(scales, axis=1)).astype(jnp.bfloat16)
+            pen_ref[pl.ds(line0 + tile * per_tile + part, 1), :] = pen[:, part * LANES : (part + 1) * LANES]
+        row_gap = jac_live * jnp.sum(field[p_size : p_size + SUB], axis=0, keepdims=True)
+        slot = line_of(slot_ref, line0 + tile * per_tile, per_tile)
+        spread = jnp.where(hi_id == (slot >> 7), row_gap, 0.0)
+        left = jnp.concatenate(split3(spread), axis=0)
+        right = jnp.where(lo_id == (slot & (LANES - 1)), 1.0, 0.0).astype(jnp.bfloat16)
+        got = lax.dot_general(
+            left, right, (((1,), (1,)), ((), ())), preferred_element_type=jnp.float32
+        )
+        seg_total = seg_total + (
+            got[0:PAD_GROUPS] + got[PAD_GROUPS : 2 * PAD_GROUPS] + got[2 * PAD_GROUPS :]
+        )
+        field = coming
     seg_ref[...] += seg_total
 
     @pl.when(step == pl.num_programs(0) - 1)
@@ -217,9 +227,9 @@
     live_ref, qw_ref, slot_ref, code_ref, key_ref, pen_ref, jac_ref, seg_ref, over_pen, over_key,
     out_pen, out_key, out_gap, out_mean,
     lane_lo, lane_pen, lane_key, accs_pen, accs_key,
-    sp_f, sp_i, ow_f, ow_i, tot_d, tot_r, tot_s,
-    spill_f, spill_i, spill_t, own_f, own_i, own_t,
-    s_spf, r_spf, s_spi, r_spi, s_owf, r_owf, s_owi, r_owi, s_td, r_td, s_tr, r_tr,
+    sp_f, sp_i, ow_f, ow_i, tot_d, tot_s,
+    spill_f, spill_i, own_f, own_i,
+    s_spf, r_spf, s_spi, r_spi, s_owf, r_owf, s_owi, r_owi, s_td, r_td,
 ):
     dom = lax.axis_index("dom")
     rep = lax.axis_index("rep")
@@ -233,16 +243,18 @@
     def greet(d, r):
         pl.semaphore_signal(barrier, inc=1, device_id=dev(d, r), device_id_type=MESH)
 
-    for j in range(1, n_rep):
-        greet(dom, rep + j)
-        greet(dom + 1, rep + j)
-        greet(dom - 1, rep + j)
-
-    def greet_dom(j, carry):
-        greet(dom + j, rep)
+    count = n_dom * n_rep
+    me = dom * n_rep + rep
+
+    def peer(j):
+        flat = lax.rem(me + j, count)
+        return lax.div(flat, n_rep), lax.rem(flat, n_rep)
+
+    def greet_peer(j, carry):
+        greet(*peer(j))
         return carry
 
-    lax.fori_loop(1, n_dom, greet_dom, 0)
+    lax.fori_loop(1, count, greet_peer, 0)
 
     live_count = live_ref[0]
     row_id = (
@@ -255,28 +267,20 @@
     total_area = jnp.sum(
         jnp.sum(area_rows, axis=0, keepdims=True), axis=1, keepdims=True
     ) * jnp.sum(qw_ref[...], axis=1, keepdims=True)
-    sub = lax.broadcasted_iota(jnp.int32, (SUB, LANES), 0)
-    pair = jnp.where(sub == 0, total_gap, jnp.where(sub == 1, total_area, 0.0))
+    lane = lax.broadcasted_iota(jnp.int32, (1, LANES), 1)
+    pair = jnp.where(lane == 0, total_gap, jnp.where(lane == 1, total_area, 0.0))
     tot_s[...] = pair
-    tot_d[dom] = pair
-
-    def tot_dom(j):
-        return pltpu.make_async_remote_copy(
-            src_ref=tot_s, dst_ref=tot_d.at[dom],
-            send_sem=s_td.at[j], recv_sem=r_td.at[dom],
-            device_id=dev(dom + j, rep), device_id_type=MESH,
-        )
-
-    def tot_dom_in(j):
-        source = lax.rem(dom - j + n_dom, n_dom)
+    tot_d[me] = pair
+
+    def tot_copy(j, source):
         return pltpu.make_async_remote_copy(
             src_ref=tot_s, dst_ref=tot_d.at[source],
             send_sem=s_td.at[j], recv_sem=r_td.at[source],
-            device_id=dev(dom + j, rep), device_id_type=MESH,
+            device_id=dev(*peer(j)), device_id_type=MESH,
         )
 
     def start_tot(j, carry):
-        tot_dom(j).start()
+        tot_copy(j, me).start()
         return carry
 
     def gather_group(g):
@@ -308,9 +312,9 @@
 
     lax.fori_loop(OWN_GROUPS, GROUPS, spill_group, 0)
 
-    pl.semaphore_wait(barrier, 3 * (n_rep - 1) + n_dom - 1)
-
-    lax.fori_loop(1, n_dom, start_tot, 0)
+    pl.semaphore_wait(barrier, count - 1)
+
+    lax.fori_loop(1, count, start_tot, 0)
 
     def spill_copy(j, source):
         return (
@@ -363,38 +367,20 @@
     ow_f[rep] = own_f[...]
     ow_i[rep] = own_i[...]
 
+    def encode(rank, face):
+        return jnp.where(rank < 0, KEY_LOW, ((rank - 2) << 30) + (FACE_MASK - face))
+
     def wait_tot(j, carry):
-        tot_dom_in(j).wait_recv()
+        tot_copy(j, lax.rem(me - j + count, count)).wait_recv()
         return carry
 
-    lax.fori_loop(1, n_dom, wait_tot, 0)
+    lax.fori_loop(1, count, wait_tot, 0)
 
     def add_tot(j, total):
         return total + tot_d[j]
 
-    dom_total = lax.fori_loop(0, n_dom, add_tot, jnp.zeros((SUB, LANES), jnp.float32))
-    own_t[...] = dom_total
-    tot_r[rep] = dom_total
-
-    def rep_tot(j, source):
-        return pltpu.make_async_remote_copy(
-            src_ref=own_t, dst_ref=tot_r.at[source],
-            send_sem=s_tr.at[j], recv_sem=r_tr.at[source],
-            device_id=dev(dom, rep + j), device_id_type=MESH,
-        )
-
-    for j in range(1, n_rep):
-        rep_tot(j, rep).start()
-
-    def encode(rank, face):
-        return jnp.where(rank < 0, KEY_LOW, ((rank - 2) << 30) + (FACE_MASK - face))
-
-    for j in range(1, n_rep):
-        rep_tot(j, lax.rem(rep - j + n_rep, n_rep)).wait_recv()
-    whole = tot_r[0]
-    for r in range(1, n_rep):
-        whole = whole + tot_r[r]
-    out_mean[0] = jnp.sum(whole[0:1, 0:1]) / jnp.sum(whole[1:2, 0:1])
+    whole = lax.fori_loop(0, count, add_tot, jnp.zeros((1, LANES), jnp.float32))
+    out_mean[0] = jnp.sum(whole[:, 0:1]) / jnp.sum(whole[:, 1:2])
 
     for j in range(n_rep):
         for copy in spill_copy(j, lax.rem(rep - j + n_rep, n_rep)):
@@ -419,12 +405,11 @@
     out_gap[...] = gap_o + gap_s
 
     def end_tot(j, carry):
-        tot_dom(j).wait_send()
+        tot_copy(j, me).wait_send()
         return carry
 
-    lax.fori_loop(1, n_dom, end_tot, 0)
+    lax.fori_loop(1, count, end_tot, 0)
     for j in range(1, n_rep):
-        rep_tot(j, rep).wait_send()
         for copy in own_copy(j, rep):
             copy.wait_send()
     for j in range(n_rep):
@@ -476,9 +461,8 @@
         ],
         out_specs=(wide, whole, padded, whole, whole, padded, padded),
         scratch_shapes=[
-            pltpu.VMEM((p_size + 16, 2 * k_size), jnp.bfloat16),
-            pltpu.VMEM((p_size, LANES), jnp.float32),
-            pltpu.VMEM((SUB, LANES), jnp.float32),
+            pltpu.VMEM((p_size + 16, 2 * k_size + 16), jnp.bfloat16),
+            pltpu.VMEM((2 * k_size, p_size), jnp.bfloat16),
             lane_packs,
             *lane_accs,
         ],
@@ -525,18 +509,15 @@
                 pltpu.VMEM((n_rep,) + tile_f, jnp.int32),
                 pltpu.VMEM((n_rep,) + tile_f, jnp.float32),
                 pltpu.VMEM((n_rep,) + tile_f, jnp.int32),
-                pltpu.VMEM((n_dom, SUB, LANES), jnp.float32),
-                pltpu.VMEM((n_rep, SUB, LANES), jnp.float32),
-                pltpu.VMEM((SUB, LANES), jnp.float32),
+                pltpu.VMEM((n_dom * n_rep, 1, LANES), jnp.float32),
+                pltpu.VMEM((1, LANES), jnp.float32),
                 pltpu.VMEM(tile_f, jnp.float32),
                 pltpu.VMEM(tile_f, jnp.int32),
-                pltpu.VMEM((SUB, LANES), jnp.float32),
                 pltpu.VMEM(tile_f, jnp.float32),
                 pltpu.VMEM(tile_f, jnp.int32),
-                pltpu.VMEM((SUB, LANES), jnp.float32),
                 sems((n_rep,)), sems((n_rep,)), sems((n_rep,)), sems((n_rep,)),
                 sems((n_rep,)), sems((n_rep,)), sems((n_rep,)), sems((n_rep,)),
-                sems((n_dom,)), sems((n_dom,)), sems((n_rep,)), sems((n_rep,)),
+                sems((n_dom * n_rep,)), sems((n_dom * n_rep,)),
             ],
             compiler_params=pltpu.CompilerParams(collective_id=0, has_side_effects=True),
         )(live, qrow, slot, code, key, pen, jac, seg, over_pen, over_key)

time: 31.4 us -> 27.6 us (0.88)
  Pallas kernels: 26.2 us -> 22.3 us
    pallas_call x1, Pallas kernels: 11.4 us -> 7.18 us  [dense_call(): pl.pallas_call(dense_kernel, grid=(grid,), out_shape=(jax.ShapeDtypeStruc...]
    pallas_call x1, Pallas kernels: 14.7 us -> 15.2 us  [shards(): pl.pallas_call(functools.partial(merge_kernel, n_dom, n_rep), out_shape=(...]
where the time goes in v4:
time: 27.6 us; the launch traced here: 27.3 us
  Pallas kernels  22.3 us (81%)
  between operations  2.99 us (11%)
  other arithmetic  1.2 us (4%)
  local copies, waits for them, and re-layouts  0.76 us (3%)
    pallas_call x1, Pallas kernels, shards(): pl.pallas_call(functools.partial(merge_kernel, n_dom, n_rep), out_shape=(...  15.2 us
    pallas_call x1, Pallas kernels, dense_call(): pl.pallas_call(dense_kernel, grid=(grid,), out_shape=(jax.ShapeDtypeStruc...  7.18 us
    unnamed x6, local copies, waits for them, and re-layouts  0.76 us
    select_n x1, other arithmetic, shards(): seg_gap = jnp.where(none, 0.0, gap_sum)  0.6 us
    select_n x1, other arithmetic, shards(): seg_face = jnp.where(none, -1, FACE_MASK - (best_key & FACE_MASK))  0.6 us

profile of v4, /device:TPU:0, one launch (start us, length us, event | category | flops | bytes accessed | tf_op | source)
XLA Modules:
  0.0 27.3 jit_solution(2840053227821254959)
XLA Ops:
  1.3 7.2 %shard_map.146 = (bf16[64,8192]{1,0:T(8,128)(2,1)}, f32[64,128]{1,0:T(8,128)}, f32[16,128]{1,0:T(8,128)}, s32[64,128]{1,0:T(8,128)}, s32[64,128]{1,0:T(8,128)}, /*index=5*/f32[16,128]{1,0:T(8,128)}, s32[16,128]{1,0:T(8,128)}) custom-call(s32[1]{0:T(128)S(6)} %copy.17.live_ref, bf16[64,256]{1,0:T(8,128)(2,1)} %ns_ref.1, bf16[64,256]{1,0:T(8,128)(2,1)} %nm_ref.1, ...), custom_call_target="tpu_custom_call" | custom-call | tf_op jit(solution)/shard_map/pallas_call | solution.py:446
  8.5 15.2 %shard_map.147 = (f32[8,128]{1,0:T(8,128)}, s32[8,128]{1,0:T(8,128)}, f32[8,128]{1,0:T(8,128)}, f32[1]{0:T(128)}) custom-call(s32[1]{0:T(128)S(6)} %copy.17.live_ref, f32[1,256]{1,0:T(1,128)} %bitcast.28, s32[64,128]{1,0:T(8,128)} %bitcast.23, s32[64,128]{1,0:T(8,128)} %get-tuple-element.17.code_ref, s32[64,128]{1,0:T(8,128)} %get-tuple-element.18.key_ref, ...), custom_call_target="tpu_custom_call" | custom-call | tf_op jit(solution)/shard_map/pallas_call | solution.py:495
  23.6 0.0 copy-start.1
  23.6 0.0 copy-start
  23.7 0.7 %copy-done.1 = s32[8,128]{1,0:T(8,128)S(1)} copy-done((s32[8,128]{1,0:T(8,128)S(1)}, s32[8,128]{1,0:T(8,128)}, u32[]{:S(2)}) %copy-start.1) | copy-done | bytes 4120
  24.3 0.0 copy-done
  24.3 0.0 copy-start.2
  24.3 0.6 %bitcast_select_fusion.1 = s32[1024]{0:T(1024)} fusion(s32[8,128]{1,0:T(8,128)S(1)} %copy-done.1, f32[8,128]{1,0:T(8,128)S(1)} %copy-done), kind=kLoop, calls=%fused_computation.1 | loop fusion | flops 4096 | bytes 12288 | tf_op jit(solution)/shard_map/jit(_where)/select_n | solution.py:527
  24.9 0.1 copy-done.2
  25.0 0.6 %bitcast_select_fusion = (f32[1024]{0:T(1024)}, f32[1024]{0:T(1024)}) fusion(f32[8,128]{1,0:T(8,128)S(1)} %copy-done.2, f32[8,128]{1,0:T(8,128)S(1)} %copy-done), kind=kLoop, calls=%fused_computation | loop fusion | flops 3072 | bytes 16384 | tf_op jit(solution)/shard_map/jit(_where)/select_n | solution.py:528
Async XLA Ops:
  23.6 0.7 %copy-start.1 = (s32[8,128]{1,0:T(8,128)S(1)}, s32[8,128]{1,0:T(8,128)}, u32[]{:S(2)}) copy-start(s32[8,128]{1,0:T(8,128)} %get-tuple-element.24) | copy-start | bytes 12292
  23.6 0.7 %copy-start = (f32[8,128]{1,0:T(8,128)S(1)}, f32[8,128]{1,0:T(8,128)}, u32[]{:S(2)}) copy-start(f32[8,128]{1,0:T(8,128)} %get-tuple-element.23) | copy-start | bytes 12292
  24.3 0.7 %copy-start.2 = (f32[8,128]{1,0:T(8,128)S(1)}, f32[8,128]{1,0:T(8,128)}, u32[]{:S(2)}) copy-start(f32[8,128]{1,0:T(8,128)} %get-tuple-element.25) | copy-start | bytes 12292

commit v5 on v4

--- a/solution.py
+++ b/solution.py
@@ -224,8 +224,9 @@
 
 def merge_kernel(
     n_dom, n_rep,
-    live_ref, qw_ref, slot_ref, code_ref, key_ref, pen_ref, jac_ref, seg_ref, over_pen, over_key,
+    live_ref, qw_ref, slot_h, code_h, key_h, pen_h, jac_h, seg_h, over_pen_h, over_key_h,
     out_pen, out_key, out_gap, out_mean,
+    slot_ref, code_ref, key_ref, pen_ref, jac_ref, seg_ref, over_pen, over_key, s_in,
     lane_lo, lane_pen, lane_key, accs_pen, accs_key,
     sp_f, sp_i, ow_f, ow_i, tot_d, tot_s,
     spill_f, spill_i, own_f, own_i,
@@ -255,6 +256,17 @@
         return carry
 
     lax.fori_loop(1, count, greet_peer, 0)
+    loads = [
+        pltpu.make_async_copy(source, held, s_in.at[i])
+        for i, (source, held) in enumerate((
+            (slot_h, slot_ref), (code_h, code_ref), (key_h, key_ref), (pen_h, pen_ref),
+            (jac_h, jac_ref), (seg_h, seg_ref), (over_pen_h, over_pen), (over_key_h, over_key),
+        ))
+    ]
+    for copy in loads:
+        copy.start()
+    for copy in loads:
+        copy.wait()
 
     live_count = live_ref[0]
     row_id = (
@@ -415,6 +427,13 @@
     for j in range(n_rep):
         for copy in spill_copy(j, rep):
             copy.wait_send()
+
+
+def finish_kernel(pen_ref, key_ref, gap_ref, out_pen, out_face, out_gap):
+    none = pen_ref[...] < LOWEST_FILL * 0.5
+    out_pen[...] = jnp.where(none, 0.0, pen_ref[...])
+    out_face[...] = jnp.where(none, -1, FACE_MASK - (key_ref[...] & FACE_MASK))
+    out_gap[...] = jnp.where(none, 0.0, gap_ref[...])
 
 
 def lane_scratch():
@@ -500,9 +519,18 @@
                 jax.ShapeDtypeStruct((SUB, LANES), jnp.float32),
                 jax.ShapeDtypeStruct((1,), jnp.float32),
             ),
-            in_specs=[smem] + [vmem] * 9,
+            in_specs=[smem, vmem] + [pl.BlockSpec(memory_space=pl.ANY)] * 8,
             out_specs=(vmem, vmem, vmem, smem),
             scratch_shapes=[
+                pltpu.VMEM((lines, LANES), jnp.int32),
+                pltpu.VMEM((lines, LANES), jnp.int32),
+                pltpu.VMEM((lines, LANES), jnp.int32),
+                pltpu.VMEM((lines, LANES), jnp.float32),
+                pltpu.VMEM((lines, LANES), jnp.float32),
+                pltpu.VMEM((PAD_GROUPS, LANES), jnp.float32),
+                pltpu.VMEM((PAD_GROUPS, LANES), jnp.float32),
+                pltpu.VMEM((PAD_GROUPS, LANES), jnp.int32),
+                sems((8,)),
                 *lane_packs,
                 *lane_accs,
                 pltpu.VMEM((n_rep,) + tile_f, jnp.float32),
@@ -521,11 +549,17 @@
             ],
             compiler_params=pltpu.CompilerParams(collective_id=0, has_side_effects=True),
         )(live, qrow, slot, code, key, pen, jac, seg, over_pen, over_key)
-        best_pen, best_key, gap_sum = (x.reshape(SEG_DEV) for x in (best_pen, best_key, gap_sum))
-        none = best_pen < LOWEST_FILL * 0.5
-        seg_pen = jnp.where(none, 0.0, best_pen)
-        seg_face = jnp.where(none, -1, FACE_MASK - (best_key & FACE_MASK))
-        seg_gap = jnp.where(none, 0.0, gap_sum)
+        seg_pen, seg_face, seg_gap = pl.pallas_call(
+            finish_kernel,
+            out_shape=(
+                jax.ShapeDtypeStruct((SUB, LANES), jnp.float32),
+                jax.ShapeDtypeStruct((SUB, LANES), jnp.int32),
+                jax.ShapeDtypeStruct((SUB, LANES), jnp.float32),
+            ),
+            in_specs=[vmem] * 3,
+            out_specs=(vmem, vmem, vmem),
+        )(best_pen, best_key, gap_sum)
+        seg_pen, seg_face, seg_gap = (x.reshape(SEG_DEV) for x in (seg_pen, seg_face, seg_gap))
         return force, seg_pen, seg_face, seg_gap, mean.reshape(())
 
     return jax.shard_map(

time: 27.6 us -> 26.8 us (0.971); the launches traced: 27.3 us -> 26.9 us
  Pallas kernels: 22.3 us -> 23.8 us
  other arithmetic: 1.2 us -> 0 us
  local copies, waits for them, and re-layouts: 0.76 us -> 0 us
    pallas_call x0 -> x1, Pallas kernels: none -> 1.29 us  [shards(): pl.pallas_call(finish_kernel, out_shape=(jax.ShapeDtypeStruct((SUB, LANES...]
    select_n x2 -> x0, other arithmetic: 1.2 us -> none  [the longest x1 0.6 us: shards(): seg_gap = jnp.where(none, 0.0, gap_sum)]
    unnamed x6 -> x0, local copies, waits for them, and re-layouts: 0.76 us -> none
where the time goes in v5:
time: 26.8 us; the launch traced here: 26.9 us
  Pallas kernels  23.8 us (89%)
  between operations  3.05 us (11%)
    pallas_call x1, Pallas kernels, shards(): pl.pallas_call(functools.partial(merge_kernel, n_dom, n_rep), out_shape=(...  15.4 us
    pallas_call x1, Pallas kernels, dense_call(): pl.pallas_call(dense_kernel, grid=(grid,), out_shape=(jax.ShapeDtypeStruc...  7.18 us
    pallas_call x1, Pallas kernels, shards(): pl.pallas_call(finish_kernel, out_shape=(jax.ShapeDtypeStruct((SUB, LANES...  1.29 us

profile of v5, /device:TPU:0, one launch (start us, length us, event | category | flops | bytes accessed | tf_op | source)
XLA Modules:
  0.0 26.9 jit_solution(10074274661286048740)
XLA Ops:
  1.3 7.2 %shard_map.146 = (bf16[64,8192]{1,0:T(8,128)(2,1)}, f32[64,128]{1,0:T(8,128)}, f32[16,128]{1,0:T(8,128)}, s32[64,128]{1,0:T(8,128)}, s32[64,128]{1,0:T(8,128)}, /*index=5*/f32[16,128]{1,0:T(8,128)}, s32[16,128]{1,0:T(8,128)}) custom-call(s32[1]{0:T(128)S(6)} %copy.17.live_ref, bf16[64,256]{1,0:T(8,128)(2,1)} %ns_ref.1, bf16[64,256]{1,0:T(8,128)(2,1)} %nm_ref.1, ...), custom_call_target="tpu_custom_call" | custom-call | tf_op jit(solution)/shard_map/pallas_call | solution.py:465
  8.5 15.4 %shard_map.147 = (f32[8,128]{1,0:T(8,128)}, s32[8,128]{1,0:T(8,128)}, f32[8,128]{1,0:T(8,128)}, f32[1]{0:T(128)}) custom-call(s32[1]{0:T(128)S(6)} %copy.17.live_ref, f32[1,256]{1,0:T(1,128)} %bitcast.18, s32[64,128]{1,0:T(8,128)} %bitcast.13, s32[64,128]{1,0:T(8,128)} %get-tuple-element.20.code_h, s32[64,128]{1,0:T(8,128)} %get-tuple-element.21.key_h, ...), custom_call_target="tpu_custom_call" | custom-call | tf_op jit(solution)/shard_map/pallas_call | solution.py:514
  23.8 1.3 %shard_map.148 = (f32[8,128]{1,0:T(8,128)}, s32[8,128]{1,0:T(8,128)}, f32[8,128]{1,0:T(8,128)}) custom-call(f32[8,128]{1,0:T(8,128)} %get-tuple-element.26.pen_ref, s32[8,128]{1,0:T(8,128)} %get-tuple-element.27.key_ref, f32[8,128]{1,0:T(8,128)} %get-tuple-element.28.gap_ref), custom_call_target="tpu_custom_call" | custom-call | tf_op jit(solution)/shard_map/pallas_call | solution.py:552

commit v6 on v5

--- a/solution.py
+++ b/solution.py
@@ -23,7 +23,7 @@
 MESH = pl.DeviceIdType.MESH
 TILE = 256
 DEPTH = 16
-BLOCK = 2048
+BLOCK = 4096
 
 
 def split3(x):
@@ -90,7 +90,7 @@
 def dense_kernel(
     live_ref, ns_ref, nm_ref, qw_ref, sec_ref, mst_ref, off_ref, jac_ref, slot_ref,
     face_ref, rank_ref,
-    force_ref, pen_ref, seg_ref, code_ref, key_ref, over_pen, over_key,
+    force_ref, pen_ref, gap_ref, code_ref, key_ref, over_pen, over_key,
     wt_ref, nq_ref, packs, accs_pen, accs_key,
 ):
     step = pl.program_id(0)
@@ -124,7 +124,6 @@
         top = scaled.astype(jnp.bfloat16)
         low = (scaled - top.astype(jnp.float32)).astype(jnp.bfloat16)
         nq_ref[...] = jnp.concatenate([top, low], axis=0)
-        seg_ref[...] = jnp.zeros_like(seg_ref)
         over_pen[...] = jnp.full(over_pen.shape, LOWEST_FILL, jnp.float32)
         over_key[...] = jnp.full(over_key.shape, KEY_LOW, jnp.int32)
         row_id = (
@@ -154,7 +153,6 @@
     line0 = step * lines
     wt = wt_ref[...]
     nq = nq_ref[...]
-    seg_total = jnp.zeros((PAD_GROUPS, LANES), jnp.float32)
     pad_rows = wt.shape[1] - 2 * k_size
     pad_id = lax.broadcasted_iota(jnp.int32, (pad_rows, TILE), 0)
 
@@ -170,8 +168,6 @@
         return jnp.dot(wt, x, preferred_element_type=jnp.float32)
 
     row_lane = lax.broadcasted_iota(jnp.int32, (1, TILE), 1)
-    hi_id = lax.broadcasted_iota(jnp.int32, (PAD_GROUPS, TILE), 0)
-    lo_id = lax.broadcasted_iota(jnp.int32, (LANES, TILE), 0)
     tiles = rows // TILE
     field = project(0)
     for tile in range(tiles):
@@ -189,19 +185,9 @@
         for part in range(per_tile):
             pen_ref[pl.ds(line0 + tile * per_tile + part, 1), :] = pen[:, part * LANES : (part + 1) * LANES]
         row_gap = jac_live * jnp.sum(field[p_size : p_size + SUB], axis=0, keepdims=True)
-        slot = line_of(slot_ref, line0 + tile * per_tile, per_tile)
-        spread = jnp.where(hi_id == (slot >> 7), row_gap, 0.0)
-        left = jnp.concatenate(split3(spread), axis=0)
-        right = jnp.where(lo_id == (slot & (LANES - 1)), 1.0, 0.0).astype(jnp.bfloat16)
-        got = lax.dot_general(
-            left, right, (((1,), (1,)), ((), ())), preferred_element_type=jnp.float32
-        )
-        seg_total = seg_total + (
-            got[0:PAD_GROUPS] + got[PAD_GROUPS : 2 * PAD_GROUPS] + got[2 * PAD_GROUPS :]
-        )
+        for part in range(per_tile):
+            gap_ref[pl.ds(line0 + tile * per_tile + part, 1), :] = row_gap[:, part * LANES : (part + 1) * LANES]
         field = coming
-    seg_ref[...] += seg_total
-
     @pl.when(step == pl.num_programs(0) - 1)
     def _():
         def one(worst):
@@ -224,9 +210,9 @@
 
 def merge_kernel(
     n_dom, n_rep,
-    live_ref, qw_ref, slot_h, code_h, key_h, pen_h, jac_h, seg_h, over_pen_h, over_key_h,
+    live_ref, qw_ref, slot_h, code_h, key_h, pen_h, jac_h, gap_h, over_pen_h, over_key_h,
     out_pen, out_key, out_gap, out_mean,
-    slot_ref, code_ref, key_ref, pen_ref, jac_ref, seg_ref, over_pen, over_key, s_in,
+    slot_ref, code_ref, key_ref, pen_ref, jac_ref, gap_ref, over_pen, over_key, s_in, seg_ref,
     lane_lo, lane_pen, lane_key, accs_pen, accs_key,
     sp_f, sp_i, ow_f, ow_i, tot_d, tot_s,
     spill_f, spill_i, own_f, own_i,
@@ -260,7 +246,7 @@
         pltpu.make_async_copy(source, held, s_in.at[i])
         for i, (source, held) in enumerate((
             (slot_h, slot_ref), (code_h, code_ref), (key_h, key_ref), (pen_h, pen_ref),
-            (jac_h, jac_ref), (seg_h, seg_ref), (over_pen_h, over_pen), (over_key_h, over_key),
+            (jac_h, jac_ref), (gap_h, gap_ref), (over_pen_h, over_pen), (over_key_h, over_key),
         ))
     ]
     for copy in loads:
@@ -274,7 +260,7 @@
         + lax.broadcasted_iota(jnp.int32, (lines, LANES), 1)
     )
     live = row_id < live_count
-    total_gap = jnp.sum(jnp.sum(seg_ref[...], axis=0, keepdims=True), axis=1, keepdims=True)
+    total_gap = jnp.sum(jnp.sum(gap_ref[...], axis=0, keepdims=True), axis=1, keepdims=True)
     area_rows = jnp.where(live, jac_ref[...], 0.0)
     total_area = jnp.sum(
         jnp.sum(area_rows, axis=0, keepdims=True), axis=1, keepdims=True
@@ -294,6 +280,26 @@
     def start_tot(j, carry):
         tot_copy(j, me).start()
         return carry
+
+    hi_id = lax.broadcasted_iota(jnp.int32, (PAD_GROUPS, LANES), 0)
+    lo_id = lax.broadcasted_iota(jnp.int32, (LANES, LANES), 0)
+
+    def add_gaps(turn, total):
+        lefts, rights = [], []
+        for i in range(SUB):
+            at = pl.ds(turn * SUB + i, 1)
+            slot = slot_ref[at, :]
+            lefts.append(jnp.where(hi_id == (slot >> 7), gap_ref[at, :], 0.0))
+            rights.append(jnp.where(lo_id == (slot & (LANES - 1)), 1.0, 0.0).astype(jnp.bfloat16))
+        left = jnp.concatenate(split3(jnp.concatenate(lefts, axis=1)), axis=0)
+        got = lax.dot_general(
+            left, jnp.concatenate(rights, axis=1), (((1,), (1,)), ((), ())),
+            preferred_element_type=jnp.float32,
+        )
+        return total + (got[0:PAD_GROUPS] + got[PAD_GROUPS : 2 * PAD_GROUPS] + got[2 * PAD_GROUPS :])
+
+    zero = jnp.zeros((PAD_GROUPS, LANES), jnp.float32)
+    seg_ref[...] = lax.fori_loop(0, lines // SUB, add_gaps, zero)
 
     def gather_group(g):
         top, best = scan_group(
@@ -468,7 +474,7 @@
         out_shape=(
             jax.ShapeDtypeStruct((k_size, rows), jnp.bfloat16),
             jax.ShapeDtypeStruct((lines, LANES), jnp.float32),
-            jax.ShapeDtypeStruct((PAD_GROUPS, LANES), jnp.float32),
+            jax.ShapeDtypeStruct((lines, LANES), jnp.float32),
             jax.ShapeDtypeStruct((lines, LANES), jnp.int32),
             jax.ShapeDtypeStruct((lines, LANES), jnp.int32),
             jax.ShapeDtypeStruct((PAD_GROUPS, LANES), jnp.float32),
@@ -478,7 +484,7 @@
             smem, full((k_size, p_size)), full((k_size, p_size)), full((1, p_size)),
             wide, wide, line_spec, line_spec, whole, whole, whole,
         ],
-        out_specs=(wide, whole, padded, whole, whole, padded, padded),
+        out_specs=(wide, whole, whole, whole, whole, padded, padded),
         scratch_shapes=[
             pltpu.VMEM((p_size + 16, 2 * k_size + 16), jnp.bfloat16),
             pltpu.VMEM((2 * k_size, p_size), jnp.bfloat16),
@@ -504,7 +510,7 @@
         off, jac, slot, face, rank = (lined(x) for x in (off, jac, slot, face, rank))
         smem = pl.BlockSpec(memory_space=pltpu.SMEM)
         lane_packs, lane_accs = lane_scratch()
-        force, pen, seg, code, key, over_pen, over_key = dense_call(
+        force, pen, gap, code, key, over_pen, over_key = dense_call(
             live, ns, nm, qrow, sec, mst, off, jac, slot, face, rank
         )
 
@@ -527,10 +533,11 @@
                 pltpu.VMEM((lines, LANES), jnp.int32),
                 pltpu.VMEM((lines, LANES), jnp.float32),
                 pltpu.VMEM((lines, LANES), jnp.float32),
-                pltpu.VMEM((PAD_GROUPS, LANES), jnp.float32),
+                pltpu.VMEM((lines, LANES), jnp.float32),
                 pltpu.VMEM((PAD_GROUPS, LANES), jnp.float32),
                 pltpu.VMEM((PAD_GROUPS, LANES), jnp.int32),
                 sems((8,)),
+                pltpu.VMEM((PAD_GROUPS, LANES), jnp.float32),
                 *lane_packs,
                 *lane_accs,
                 pltpu.VMEM((n_rep,) + tile_f, jnp.float32),
@@ -548,7 +555,7 @@
                 sems((n_dom * n_rep,)), sems((n_dom * n_rep,)),
             ],
             compiler_params=pltpu.CompilerParams(collective_id=0, has_side_effects=True),
-        )(live, qrow, slot, code, key, pen, jac, seg, over_pen, over_key)
+        )(live, qrow, slot, code, key, pen, jac, gap, over_pen, over_key)
         seg_pen, seg_face, seg_gap = pl.pallas_call(
             finish_kernel,
             out_shape=(

time: 26.8 us -> 26.9 us (level); the launches traced: 26.9 us -> 26.6 us
  Pallas kernels: 23.8 us -> 23.5 us
    pallas_call x1, Pallas kernels: 7.18 us -> 6.47 us  [dense_call(): pl.pallas_call(dense_kernel, grid=(grid,), out_shape=(jax.ShapeDtypeStruc...]
    pallas_call x1, Pallas kernels: 15.4 us -> 15.8 us  [shards(): pl.pallas_call(functools.partial(merge_kernel, n_dom, n_rep), out_shape=(...]
where the time goes in v6:
time: 26.9 us; the launch traced here: 26.6 us
  Pallas kernels  23.5 us (87%)
  between operations  3.04 us (11%)
    pallas_call x1, Pallas kernels, shards(): pl.pallas_call(functools.partial(merge_kernel, n_dom, n_rep), out_shape=(...  15.8 us
    pallas_call x1, Pallas kernels, dense_call(): pl.pallas_call(dense_kernel, grid=(grid,), out_shape=(jax.ShapeDtypeStruc...  6.47 us
    pallas_call x1, Pallas kernels, shards(): pl.pallas_call(finish_kernel, out_shape=(jax.ShapeDtypeStruct((SUB, LANES...  1.29 us

profile of v6, /device:TPU:0, one launch (start us, length us, event | category | flops | bytes accessed | tf_op | source)
XLA Modules:
  0.0 26.6 jit_solution(9843233508291080511)
XLA Ops:
  1.3 6.5 %shard_map.146 = (bf16[64,8192]{1,0:T(8,128)(2,1)}, f32[64,128]{1,0:T(8,128)}, f32[64,128]{1,0:T(8,128)}, s32[64,128]{1,0:T(8,128)}, s32[64,128]{1,0:T(8,128)}, /*index=5*/f32[16,128]{1,0:T(8,128)}, s32[16,128]{1,0:T(8,128)}) custom-call(s32[1]{0:T(128)S(6)} %copy.17.live_ref, bf16[64,256]{1,0:T(8,128)(2,1)} %ns_ref.1, bf16[64,256]{1,0:T(8,128)(2,1)} %nm_ref.1, ...), custom_call_target="tpu_custom_call" | custom-call | tf_op jit(solution)/shard_map/pallas_call | solution.py:471
  7.8 15.8 %shard_map.147 = (f32[8,128]{1,0:T(8,128)}, s32[8,128]{1,0:T(8,128)}, f32[8,128]{1,0:T(8,128)}, f32[1]{0:T(128)}) custom-call(s32[1]{0:T(128)S(6)} %copy.17.live_ref, f32[1,256]{1,0:T(1,128)} %bitcast.18, s32[64,128]{1,0:T(8,128)} %bitcast.13, s32[64,128]{1,0:T(8,128)} %get-tuple-element.20.code_h, s32[64,128]{1,0:T(8,128)} %get-tuple-element.21.key_h, ...), custom_call_target="tpu_custom_call" | custom-call | tf_op jit(solution)/shard_map/pallas_call | solution.py:520
  23.5 1.3 %shard_map.148 = (f32[8,128]{1,0:T(8,128)}, s32[8,128]{1,0:T(8,128)}, f32[8,128]{1,0:T(8,128)}) custom-call(f32[8,128]{1,0:T(8,128)} %get-tuple-element.26.pen_ref, s32[8,128]{1,0:T(8,128)} %get-tuple-element.27.key_ref, f32[8,128]{1,0:T(8,128)} %get-tuple-element.28.gap_ref), custom_call_target="tpu_custom_call" | custom-call | tf_op jit(solution)/shard_map/pallas_call | solution.py:559
